TPU v7x, 256 devices: a whole 4x4x8 slice. The times are simulated.
256 devices in a mesh: tm: 16 (over z, core), rows: 16 (over y, x).
Axes of the slice: x: 4, y: 4, z: 8, core: 2. Of those that a mesh axis runs over, the one named last changes fastest.
Arguments:
- frames_in: bfloat16 [32, 64, 120, 128], P('tm', 'rows'), may hold values from -25 to 25, as said below
- norm_gain: float32 [128], replicated, may hold values from 0.25 to 1.75
- norm_bias: float32 [128], replicated, may hold values from -0.5 to 0.5
- conv_weight: bfloat16 [3, 3, 3, 128, 128], replicated, may hold values from -0.109375 to 0.109375
- cotangent: bfloat16 [32, 64, 120, 128], P('tm', 'rows'), may hold values from -6 to 6
Outputs:
- output_frames: bfloat16 [32, 64, 120, 128], P('tm', 'rows')
- input_grad: bfloat16 [32, 64, 120, 128], P('tm', 'rows')
- weight_grad: float32 [128, 3456], P('rows')
- gain_grad: float32 [128], replicated
- bias_grad: float32 [128], replicated
Inputs may be any that keep to these rules, and one draw needn't show every extreme that they name: Entries of frames_in lie within 25 in magnitude.
All inputs are finite; a program needn't handle non-finite values.
Results may differ from a plain program's by a relative error of at most 0.0042.
Values may be sent and summed in bfloat16 or wider, within the bound.
A program may use at most 64 MiB of HBM per device.

v0:
```python
import math

import jax
import jax.numpy as jnp
from jax import lax
from jax.sharding import Mesh
from jax.sharding import PartitionSpec as P

G = 32
TM = ("tm_0", "tm_1")
ROWS = ("rows_0", "rows_1")


EPSILON = 1e-06


def from_behind(block, axis, distance):
    devices = range(lax.axis_size(axis))
    route = [(i - distance, i) for i in devices if i - distance in devices]
    return lax.ppermute(block, axis, route)


def padded_2(block, sides, width):
    for axis, dim in sides:
        count = lax.axis_size(axis)
        forward = [(i, i + 1) for i in range(count - 1)]
        backward = [(target, source) for source, target in forward]
        low = lax.ppermute(
            lax.slice_in_dim(block, block.shape[dim] - width, None, axis=dim), axis, forward
        )
        high = lax.ppermute(lax.slice_in_dim(block, 0, width, axis=dim), axis, backward)
        block = jnp.concatenate([low, block, high], axis=dim)
    return block


def sent_to_all(value, axis):
    devices = lax.axis_size(axis)
    return lax.all_to_all(
        jnp.broadcast_to(value[None], (devices, *value.shape)), axis, 0, 0, tiled=True
    )


def taken_together(value, axis):
    return sent_to_all(value, axis).sum(axis=0)


def by_axis(value, axes):
    far, near = axes
    nearer = taken_together(value, near)
    return taken_together(nearer, far)


def packed_total(arrays, axis):
    flat, at, finished = (jnp.concatenate([a.reshape(-1) for a in arrays]), 0, [])
    running = by_axis(flat, axis)
    for a in arrays:
        finished.append(running[at : at + a.size].reshape(a.shape))
        at += a.size
    return tuple(finished)


def cut_along(value, dim, devices):
    before, after = (value.shape[:dim], value.shape[dim + 1 :])
    return jnp.moveaxis(value.reshape(*before, devices, -1, *after), dim, 0)


def sent_and_summed(value, axis, dim):
    parts = cut_along(value, dim, lax.axis_size(axis))
    arrived = lax.all_to_all(parts, axis, split_axis=0, concat_axis=0, tiled=True)
    return arrived.sum(axis=0)


def total_of_pieces(value, axis):
    return lax.all_gather(value, axis).sum(0)


def group_expand(per_channel, groups):
    channels = per_channel.shape[0]
    return jnp.repeat(
        per_channel.reshape(groups, channels // groups).sum(axis=1), channels // groups
    )


def per_device(frames_in, norm_gain, norm_bias, conv_weight, cotangent):
    frames, band_rows, columns, channels = frames_in.shape
    groups = G
    all_pixels = frames * lax.axis_size(TM) * band_rows * lax.axis_size(ROWS) * columns
    total_cells = all_pixels * (channels // groups)
    values = frames_in.astype(jnp.float32)
    cached = from_behind(frames_in, TM, 1)
    stacked = jnp.concatenate([cached, frames_in], axis=0)
    margin_in = padded_2(stacked, ((ROWS, 1),), 1)
    channel_sum = jnp.sum(values, axis=(0, 1, 2))
    channel_sq = jnp.sum(values * values, axis=(0, 1, 2))
    group_sum = channel_sum.reshape(groups, channels // groups).sum(axis=1)
    group_sq = channel_sq.reshape(groups, channels // groups).sum(axis=1)
    group_sum, group_sq = packed_total(
        (group_sum, group_sq), (("tm_0", "tm_1", "rows_0"), "rows_1")
    )
    group_mean = jnp.repeat(group_sum, channels // groups) / total_cells
    variance = jnp.repeat(group_sq, channels // groups) / total_cells - group_mean * group_mean
    inverse_std = lax.rsqrt(variance + EPSILON)
    normed = (values - group_mean) * inverse_std
    preact = normed * norm_gain + norm_bias
    margin_vals = (margin_in.astype(jnp.float32) - group_mean) * inverse_std * norm_gain + norm_bias
    margin_act = jax.nn.silu(margin_vals)
    time_keep = (jnp.arange(frames + 2) >= 2) | (lax.axis_index(TM) > 0)
    row_index = jnp.arange(band_rows + 2)
    row_keep = ((row_index >= 1) | (lax.axis_index(ROWS) > 0)) & (
        (row_index <= band_rows) | (lax.axis_index(ROWS) < lax.axis_size(ROWS) - 1)
    )
    keep_mask = time_keep[:, None] & row_keep[None, :]
    padded = jnp.where(keep_mask[:, :, None, None], margin_act, 0.0).astype(jnp.bfloat16)
    padded = jnp.pad(padded, ((0, 0), (0, 0), (1, 1), (0, 0)))
    pixels = frames * band_rows * columns
    conv_sum = jnp.zeros((pixels, channels), jnp.float32)
    for time_off in range(3):
        for row_off in range(3):
            for col_off in range(3):
                window = padded[
                    time_off : time_off + frames,
                    row_off : row_off + band_rows,
                    col_off : col_off + columns,
                ].reshape(pixels, channels)
                conv_sum = conv_sum + jnp.dot(
                    window,
                    conv_weight[time_off, row_off, col_off],
                    preferred_element_type=jnp.float32,
                )
    output_frames = (values + conv_sum.reshape(values.shape)).astype(jnp.bfloat16)
    grad_next = from_behind(cotangent, TM, -1)
    grad_stack = jnp.concatenate([cotangent, grad_next], axis=0)
    grad_padded = padded_2(grad_stack, ((ROWS, 1),), 1)
    grad_padded = jnp.pad(grad_padded, ((0, 0), (0, 0), (1, 1), (0, 0)))
    grad_act = jnp.zeros((pixels, channels), jnp.float32)
    for time_off in range(3):
        for row_off in range(3):
            for col_off in range(3):
                grad_window = grad_padded[
                    time_off : time_off + frames,
                    row_off : row_off + band_rows,
                    col_off : col_off + columns,
                ].reshape(pixels, channels)
                flipped = conv_weight[2 - time_off, 2 - row_off, 2 - col_off].T
                grad_act = grad_act + jnp.dot(
                    grad_window, flipped, preferred_element_type=jnp.float32
                )
    grad_flat = cotangent.reshape(pixels, channels)
    pieces = []
    for time_off in range(3):
        for row_off in range(3):
            for col_off in range(3):
                window = padded[
                    time_off : time_off + frames,
                    row_off : row_off + band_rows,
                    col_off : col_off + columns,
                ].reshape(pixels, channels)
                pieces.append(
                    lax.dot_general(
                        grad_flat,
                        window,
                        (((0,), (0,)), ((), ())),
                        preferred_element_type=jnp.float32,
                    )
                )
    band_part = sent_and_summed(jnp.concatenate(pieces, axis=1), ROWS, 0)
    weight_sum = total_of_pieces(band_part, TM)
    weight_grad = weight_sum * (1.0 / math.sqrt(all_pixels))
    sigmoid_v = jax.nn.sigmoid(preact)
    grad_pre = grad_act.reshape(values.shape) * sigmoid_v * (1.0 + preact * (1.0 - sigmoid_v))
    gain_part = jnp.sum(grad_pre * normed, axis=(0, 1, 2))
    bias_part = jnp.sum(grad_pre, axis=(0, 1, 2))
    gain_grad, bias_grad = packed_total(
        (gain_part, bias_part), (("tm_0", "tm_1", "rows_0"), "rows_1")
    )
    mean_dn = group_expand(norm_gain * bias_grad, groups) / total_cells
    mean_dnn = group_expand(norm_gain * gain_grad, groups) / total_cells
    input_grad = inverse_std * (
        grad_pre * norm_gain - mean_dn - normed * mean_dnn
    ) + cotangent.astype(jnp.float32)
    return (output_frames, input_grad.astype(jnp.bfloat16), weight_grad, gain_grad, bias_grad)


def solution(mesh):
    torus = Mesh(mesh.devices.reshape(8, 2, 4, 4), ("tm_0", "tm_1", "rows_0", "rows_1"))
    placed = (P(TM, ROWS, None, None), P(), P(), P(), P(TM, ROWS, None, None))
    return jax.shard_map(
        per_device,
        mesh=torus,
        in_specs=placed,
        out_specs=(P(TM, ROWS, None, None), P(TM, ROWS, None, None), P(ROWS, None), P(), P()),
        check_vma=False,
    )
```

profile of v0, /device:TPU:1, one launch (start us, length us, event | category | flops | bytes accessed | tf_op | source)
XLA Modules:
  0.0 153.8 jit_solution(1249327753380067748)
XLA Ops:
  7.2 5.1 %collective-permute-start = (bf16[2,4,120,128]{3,2,1,0:T(8,128)(2,1)}, bf16[2,4,120,128]{3,2,1,0:T(8,128)(2,1)S(1)}, u32[]{:S(2)}, u32[]{:S(2)}) collective-permute-start(bf16[2,4,120,128]{3,2,1,0:T(8,128)(2,1)} %param.5), channel_id=1, source_target_pairs={{0,16},{16,32},{32,48},{48,64},{64,80},{80,96},{96,112},{112,128},... | collective-permute-start | bytes 737288 | tf_op jit(solution)/shard_map/ppermute | solution.py:20
  12.3 1.1 convert_reduce_fusion
  13.9 0.6 broadcast_in_dim.29
  14.5 4.0 %all-to-all-start = ((f32[4,1,64]{2,1,0:T(1,128)}), f32[4,1,64]{2,1,0:T(1,128)S(1)}, u32[]{:S(2)}, u32[]{:S(2)}) async-start(f32[4,1,64]{2,1,0:T(1,128)} %broadcast_in_dim.29), calls=%async_computation | async-start | bytes 4096 | tf_op jit(solution)/shard_map/all_to_all | solution.py:38
  18.5 1.9 %collective-permute-start.3 = (bf16[2,4,120,128]{3,2,1,0:T(8,128)(2,1)}, bf16[2,4,120,128]{3,2,1,0:T(8,128)(2,1)S(1)}, u32[]{:S(2)}, u32[]{:S(2)}) collective-permute-start(bf16[2,4,120,128]{3,2,1,0:T(8,128)(2,1)} %param.9), channel_id=1, source_target_pairs={{16,0},{32,16},{48,32},{64,48},{80,64},{96,80},{112,96},{128,112},... | collective-permute-start | bytes 737288 | tf_op jit(solution)/shard_map/ppermute | solution.py:20
  20.5 2.0 %all-to-all-done = f32[4,1,64]{2,1,0:T(1,128)S(1)} async-done(((f32[4,1,64]{2,1,0:T(1,128)}), f32[4,1,64]{2,1,0:T(1,128)S(1)}, u32[]{:S(2)}, u32[]{:S(2)}) %all-to-all-start) | async-done | bytes 1056 | tf_op jit(solution)/shard_map/all_to_all | solution.py:38
  22.6 0.6 broadcast_in_dim.30
  23.2 11.6 %all-to-all-start.1 = ((f32[64,1,64]{2,1,0:T(1,128)}), f32[64,1,64]{2,1,0:T(1,128)S(1)}, u32[]{:S(2)}, u32[]{:S(2)}) async-start(f32[64,1,64]{2,1,0:T(1,128)} %broadcast_in_dim.30), calls=%async_computation.1 | async-start | bytes 65536 | tf_op jit(solution)/shard_map/all_to_all | solution.py:38
  34.8 1.0 constant_dynamic-update-slice_fusion.3
  35.7 8.1 %all-to-all-done.1 = f32[64,1,64]{2,1,0:T(1,128)S(1)} async-done(((f32[64,1,64]{2,1,0:T(1,128)}), f32[64,1,64]{2,1,0:T(1,128)S(1)}, u32[]{:S(2)}, u32[]{:S(2)}) %all-to-all-start.1) | async-done | bytes 16416 | tf_op jit(solution)/shard_map/all_to_all | solution.py:38
  44.4 1.0 constant_dynamic-update-slice_fusion
  45.5 2.9 %collective-permute-start.1 = (bf16[4,1,120,128]{3,2,1,0:T(8,128)(2,1)S(1)}, bf16[4,1,120,128]{3,2,1,0:T(8,128)(2,1)S(1)}, u32[]{:S(2)}, u32[]{:S(2)}) collective-permute-start(bf16[4,1,120,128]{3,2,1,0:T(8,128)(2,1)S(1)} %get-tuple-element.71), channel_id=1, source_target_pairs={{0,1},{1,2},{2,3},{3,4},{4,5},{5,6},{6,7},{7,8},{8,9},{9,10},{10,1... | collective-permute-start | bytes 368648 | tf_op jit(solution)/shard_map/ppermute | solution.py:28
  48.3 1.3 collective-permute-start.2
  49.7 0.7 fusion.215
  50.4 4.7 %collective-permute-start.4 = (bf16[4,1,120,128]{3,2,1,0:T(8,128)(2,1)}, bf16[4,1,120,128]{3,2,1,0:T(8,128)(2,1)}, u32[]{:S(2)}, u32[]{:S(2)}) collective-permute-start(bf16[4,1,120,128]{3,2,1,0:T(8,128)(2,1)} %get-tuple-element.69), channel_id=1, source_target_pairs={{0,1},{1,2},{2,3},{3,4},{4,5},{5,6},{6,7},{7,8},{8,9},{9,10},{10,1... | collective-permute-start | bytes 368648 | tf_op jit(solution)/shard_map/ppermute | solution.py:28
  55.1 1.3 collective-permute-start.5
  56.4 0.6 select_convert_fusion
  57.3 1.1 fusion.214
  58.4 1.6 %pad_slice_fusion.8 = (bf16[2,4,120,128]{3,2,1,0:T(8,128)(2,1)}, bf16[2,4,120,128]{3,2,1,0:T(8,128)(2,1)}, bf16[2,4,120,128]{3,2,1,0:T(8,128)(2,1)}, bf16[2,4,12...) fusion(bf16[4,6,120,128]{3,2,1,0:T(8,128)(2,1)S(1)} %select_con, ...), kind=kLoop, calls=%fused_computation.318 | loop fusion | bytes 3440640 | tf_op jit(solution)/shard_map/slice | solution.py:120
  60.3 0.3 fusion.30
  60.6 0.3 fusion.29
  61.1 0.3 fusion.28
  61.4 0.3 fusion.27
  61.9 0.3 fusion.26
  62.8 0.3 fusion.24
  63.0 0.3 fusion.23
  63.6 0.3 fusion.22
  63.9 0.3 fusion.21
  64.4 0.3 fusion.20
  64.7 0.3 fusion.19
  66.1 0.3 fusion.16
  66.4 0.3 fusion.15
  66.9 0.3 fusion.14
  67.2 2.0 %copy.16 = f32[128,3456]{1,0:T(8,128)} copy(f32[128,3456]{0,1:T(8,128)S(1)} %fusion.14) | data formatting | bytes 3538944 | tf_op jit(solution)/shard_map/concatenate | solution.py:166
  69.2 7.1 %all-to-all-start.4 = ((f32[16,8,3456]{2,1,0:T(8,128)}), f32[16,8,3456]{2,1,0:T(8,128)S(1)}, u32[]{:S(2)}, u32[]{:S(2)}) async-start(f32[16,8,3456]{2,1,0:T(8,128)} %bitcast.166), calls=%async_computation.4 | async-start | bytes 3538944 | tf_op jit(solution)/shard_map/all_to_all | solution.py:69
  76.3 1.2 fusion.36
  77.6 0.6 fusion.213
  78.2 0.6 copy-done.2
  80.1 1.1 pad_maximum_fusion
  86.3 0.4 copy-done.1
  86.8 0.3 fusion.51
  91.3 1.5 pad_slice_fusion.9
  93.4 5.4 %all-to-all-done.4 = f32[16,8,3456]{2,1,0:T(8,128)S(1)} async-done(((f32[16,8,3456]{2,1,0:T(8,128)}), f32[16,8,3456]{2,1,0:T(8,128)S(1)}, u32[]{:S(2)}, u32[]{:S(2)}) %all-to-all-start.4) | async-done | bytes 1769504 | tf_op jit(solution)/shard_map/all_to_all | solution.py:69
  98.8 0.6 broadcast_in_dim.34
  99.4 4.4 %all-to-all-start.2 = ((f32[4,1,256]{2,1,0:T(1,128)}), f32[4,1,256]{2,1,0:T(1,128)S(1)}, u32[]{:S(2)}, u32[]{:S(2)}) async-start(f32[4,1,256]{2,1,0:T(1,128)} %broadcast_in_dim.34), calls=%async_computation.2 | async-start | bytes 8192 | tf_op jit(solution)/shard_map/all_to_all | solution.py:38
  103.8 0.7 reduce_sum.138
  104.6 1.2 convolution_add_fusion.31
  105.8 1.2 convolution_add_fusion.30
  107.0 1.0 convolution_add_fusion.29
  108.1 1.0 convolution_add_fusion.28
  109.1 1.0 convolution_add_fusion.27
  110.1 1.0 convolution_add_fusion.26
  111.2 1.0 convolution_add_fusion.25
  112.2 1.0 convolution_add_fusion.24
  113.2 1.0 convolution_add_fusion.23
  114.2 0.7 broadcast_in_dim.35
  114.8 7.4 %all-to-all-start.3 = ((f32[64,1,256]{2,1,0:T(1,128)}), f32[64,1,256]{2,1,0:T(1,128)S(1)}, u32[]{:S(2)}, u32[]{:S(2)}) async-start(f32[64,1,256]{2,1,0:T(1,128)} %broadcast_in_dim.35), calls=%async_computation.3 | async-start | bytes 131072 | tf_op jit(solution)/shard_map/all_to_all | solution.py:38
  122.3 1.0 convolution_add_fusion.22
  123.2 8.4 %all-to-all-done.3 = f32[64,1,256]{2,1,0:T(1,128)S(1)} async-done(((f32[64,1,256]{2,1,0:T(1,128)}), f32[64,1,256]{2,1,0:T(1,128)S(1)}, u32[]{:S(2)}, u32[]{:S(2)}) %all-to-all-start.3) | async-done | bytes 65568 | tf_op jit(solution)/shard_map/all_to_all | solution.py:38
  131.7 0.5 fusion.210
  133.1 1.0 fusion.55
  134.1 10.6 %all-gather.3.cloned.1.call-done = f32[128,3456]{1,0:T(8,128)} async-done(((f32[8,3456]{1,0:T(8,128)}), f32[128,3456]{1,0:T(8,128)}) %all-gather.3.cloned.1.call-update) | async-done | bytes 1769488 | tf_op jit(solution)/shard_map/all_gather | solution.py:74
  144.7 1.6 %bitcast_reduce_fusion = f32[8,3456]{1,0:T(8,128)S(1)} fusion(f32[128,3456]{1,0:T(8,128)} %all-gather.3.cloned.1.call-done), kind=kLoop, calls=%fused_computation.2 | loop fusion | flops 414720 | bytes 1880064 | tf_op jit(solution)/shard_map/reduce_sum | solution.py:74
  146.3 0.7 broadcast_multiply_fusion
  (150 shorter events, 16.6 us)
Async XLA Ops:
  7.2 49.2 %copy-start.25 = (f32[128]{0:T(128)S(1)}, f32[128]{0:T(128)}, u32[]{:S(2)}) copy-start(f32[128]{0:T(128)} %param.6) | copy-start | bytes 1540
  7.2 49.2 %copy-start.26 = (f32[128]{0:T(128)S(1)}, f32[128]{0:T(128)}, u32[]{:S(2)}) copy-start(f32[128]{0:T(128)} %param.7) | copy-start | bytes 1540
  7.2 37.2 %collective-permute-start = (bf16[2,4,120,128]{3,2,1,0:T(8,128)(2,1)}, bf16[2,4,120,128]{3,2,1,0:T(8,128)(2,1)S(1)}, u32[]{:S(2)}, u32[]{:S(2)}) collective-permute-start(bf16[2,4,120,128]{3,2,1,0:T(8,128)(2,1)} %param.5), channel_id=1, source_target_pairs={{0,16},{16,32},{32,48},{48,64},{64,80},{80,96},{96,112},{112,128},... | collective-permute-start | bytes 737288 | tf_op jit(solution)/shard_map/ppermute | solution.py:20
  14.5 8.1 %all-to-all-start = ((f32[4,1,64]{2,1,0:T(1,128)}), f32[4,1,64]{2,1,0:T(1,128)S(1)}, u32[]{:S(2)}, u32[]{:S(2)}) async-start(f32[4,1,64]{2,1,0:T(1,128)} %broadcast_in_dim.29), calls=%async_computation | async-start | bytes 4096 | tf_op jit(solution)/shard_map/all_to_all | solution.py:38
  18.5 31.2 %collective-permute-start.3 = (bf16[2,4,120,128]{3,2,1,0:T(8,128)(2,1)}, bf16[2,4,120,128]{3,2,1,0:T(8,128)(2,1)S(1)}, u32[]{:S(2)}, u32[]{:S(2)}) collective-permute-start(bf16[2,4,120,128]{3,2,1,0:T(8,128)(2,1)} %param.9), channel_id=1, source_target_pairs={{16,0},{32,16},{48,32},{64,48},{80,64},{96,80},{112,96},{128,112},... | collective-permute-start | bytes 737288 | tf_op jit(solution)/shard_map/ppermute | solution.py:20
  23.2 20.7 %all-to-all-start.1 = ((f32[64,1,64]{2,1,0:T(1,128)}), f32[64,1,64]{2,1,0:T(1,128)S(1)}, u32[]{:S(2)}, u32[]{:S(2)}) async-start(f32[64,1,64]{2,1,0:T(1,128)} %broadcast_in_dim.30), calls=%async_computation.1 | async-start | bytes 65536 | tf_op jit(solution)/shard_map/all_to_all | solution.py:38
  44.4 12.6 %copy-start = (bf16[2,4,120,128]{3,2,1,0:T(8,128)(2,1)S(1)}, bf16[2,4,120,128]{3,2,1,0:T(8,128)(2,1)}, u32[]{:S(2)}) copy-start(bf16[2,4,120,128]{3,2,1,0:T(8,128)(2,1)} %param.9) | copy-start | bytes 737284
  45.5 10.9 %collective-permute-start.1 = (bf16[4,1,120,128]{3,2,1,0:T(8,128)(2,1)S(1)}, bf16[4,1,120,128]{3,2,1,0:T(8,128)(2,1)S(1)}, u32[]{:S(2)}, u32[]{:S(2)}) collective-permute-start(bf16[4,1,120,128]{3,2,1,0:T(8,128)(2,1)S(1)} %get-tuple-element.71), channel_id=1, source_target_pairs={{0,1},{1,2},{2,3},{3,4},{4,5},{5,6},{6,7},{7,8},{8,9},{9,10},{10,1... | collective-permute-start | bytes 368648 | tf_op jit(solution)/shard_map/ppermute | solution.py:28
  48.3 8.0 %collective-permute-start.2 = (bf16[4,1,120,128]{3,2,1,0:T(8,128)(2,1)S(1)}, bf16[4,1,120,128]{3,2,1,0:T(8,128)(2,1)S(1)}, u32[]{:S(2)}, u32[]{:S(2)}) collective-permute-start(bf16[4,1,120,128]{3,2,1,0:T(8,128)(2,1)S(1)} %get-tuple-element.72), channel_id=1, source_target_pairs={{1,0},{2,1},{3,2},{4,3},{5,4},{6,5},{7,6},{8,7},{9,8},{10,9},{11,1... | collective-permute-start | bytes 368648 | tf_op jit(solution)/shard_map/ppermute | solution.py:31
  50.4 25.9 %collective-permute-start.4 = (bf16[4,1,120,128]{3,2,1,0:T(8,128)(2,1)}, bf16[4,1,120,128]{3,2,1,0:T(8,128)(2,1)}, u32[]{:S(2)}, u32[]{:S(2)}) collective-permute-start(bf16[4,1,120,128]{3,2,1,0:T(8,128)(2,1)} %get-tuple-element.69), channel_id=1, source_target_pairs={{0,1},{1,2},{2,3},{3,4},{4,5},{5,6},{6,7},{7,8},{8,9},{9,10},{10,1... | collective-permute-start | bytes 368648 | tf_op jit(solution)/shard_map/ppermute | solution.py:28
  55.1 21.3 %collective-permute-start.5 = (bf16[4,1,120,128]{3,2,1,0:T(8,128)(2,1)}, bf16[4,1,120,128]{3,2,1,0:T(8,128)(2,1)}, u32[]{:S(2)}, u32[]{:S(2)}) collective-permute-start(bf16[4,1,120,128]{3,2,1,0:T(8,128)(2,1)} %get-tuple-element.70), channel_id=1, source_target_pairs={{1,0},{2,1},{3,2},{4,3},{5,4},{6,5},{7,6},{8,7},{9,8},{10,9},{11,1... | collective-permute-start | bytes 368648 | tf_op jit(solution)/shard_map/ppermute | solution.py:31
  69.2 29.6 %all-to-all-start.4 = ((f32[16,8,3456]{2,1,0:T(8,128)}), f32[16,8,3456]{2,1,0:T(8,128)S(1)}, u32[]{:S(2)}, u32[]{:S(2)}) async-start(f32[16,8,3456]{2,1,0:T(8,128)} %bitcast.166), calls=%async_computation.4 | async-start | bytes 3538944 | tf_op jit(solution)/shard_map/all_to_all | solution.py:69
  77.6 1.2 copy-start.2
  77.6 1.2 copy-start.24
  85.8 0.9 copy-start.1
  86.0 1.0 copy-start.21
  86.1 1.2 copy-start.23
  86.8 1.0 copy-start.22
  87.1 1.0 copy-start.18
  87.3 1.0 copy-start.20
  87.8 1.0 copy-start.19
  88.1 1.0 copy-start.15
  88.3 1.0 copy-start.17
  88.8 1.0 copy-start.16
  89.1 1.0 copy-start.12
  89.3 1.0 copy-start.14
  89.8 1.0 copy-start.13
  90.1 1.0 copy-start.11
  99.4 14.7 %all-to-all-start.2 = ((f32[4,1,256]{2,1,0:T(1,128)}), f32[4,1,256]{2,1,0:T(1,128)S(1)}, u32[]{:S(2)}, u32[]{:S(2)}) async-start(f32[4,1,256]{2,1,0:T(1,128)} %broadcast_in_dim.34), calls=%async_computation.2 | async-start | bytes 8192 | tf_op jit(solution)/shard_map/all_to_all | solution.py:38
  103.8 40.9 %all-gather.3.cloned.1.call-start = ((), (), s32[]{:S(2)}) async-start(), calls=%async_computation.5 | async-start | bytes 1880064 | tf_op jit(solution)/shard_map/all_gather | solution.py:74
  104.5 2.5 %copy-start.8 = (bf16[2,4,120,128]{3,2,1,0:T(8,128)(2,1)S(1)}, bf16[2,4,120,128]{3,2,1,0:T(8,128)(2,1)}, u32[]{:S(2)}) copy-start(bf16[2,4,120,128]{3,2,1,0:T(8,128)(2,1)} %get-tuple-element.51) | copy-start | bytes 737284
  104.6 3.5 %copy-start.7 = (bf16[2,4,120,128]{3,2,1,0:T(8,128)(2,1)S(1)}, bf16[2,4,120,128]{3,2,1,0:T(8,128)(2,1)}, u32[]{:S(2)}) copy-start(bf16[2,4,120,128]{3,2,1,0:T(8,128)(2,1)} %get-tuple-element.47) | copy-start | bytes 737284
  105.8 3.3 %copy-start.6 = (bf16[2,4,120,128]{3,2,1,0:T(8,128)(2,1)S(1)}, bf16[2,4,120,128]{3,2,1,0:T(8,128)(2,1)}, u32[]{:S(2)}) copy-start(bf16[2,4,120,128]{3,2,1,0:T(8,128)(2,1)} %get-tuple-element.48) | copy-start | bytes 737284
  107.0 3.1 %copy-start.5 = (bf16[2,4,120,128]{3,2,1,0:T(8,128)(2,1)S(1)}, bf16[2,4,120,128]{3,2,1,0:T(8,128)(2,1)}, u32[]{:S(2)}) copy-start(bf16[2,4,120,128]{3,2,1,0:T(8,128)(2,1)} %get-tuple-element.50) | copy-start | bytes 737284
  108.1 3.1 %copy-start.4 = (bf16[2,4,120,128]{3,2,1,0:T(8,128)(2,1)S(1)}, bf16[2,4,120,128]{3,2,1,0:T(8,128)(2,1)}, u32[]{:S(2)}) copy-start(bf16[2,4,120,128]{3,2,1,0:T(8,128)(2,1)} %get-tuple-element.49) | copy-start | bytes 737284
  109.1 3.1 %copy-start.3 = (bf16[2,4,120,128]{3,2,1,0:T(8,128)(2,1)S(1)}, bf16[2,4,120,128]{3,2,1,0:T(8,128)(2,1)}, u32[]{:S(2)}) copy-start(bf16[2,4,120,128]{3,2,1,0:T(8,128)(2,1)} %get-tuple-element.42) | copy-start | bytes 737284
  110.1 3.0 %copy-start.10 = (bf16[2,4,120,128]{3,2,1,0:T(8,128)(2,1)S(1)}, bf16[2,4,120,128]{3,2,1,0:T(8,128)(2,1)}, u32[]{:S(2)}) copy-start(bf16[2,4,120,128]{3,2,1,0:T(8,128)(2,1)} %get-tuple-element.41) | copy-start | bytes 737284
  111.2 11.1 %copy-start.9 = (bf16[2,4,120,128]{3,2,1,0:T(8,128)(2,1)S(1)}, bf16[2,4,120,128]{3,2,1,0:T(8,128)(2,1)}, u32[]{:S(2)}) copy-start(bf16[2,4,120,128]{3,2,1,0:T(8,128)(2,1)} %get-tuple-element.32) | copy-start | bytes 737284
  114.8 16.8 %all-to-all-start.3 = ((f32[64,1,256]{2,1,0:T(1,128)}), f32[64,1,256]{2,1,0:T(1,128)S(1)}, u32[]{:S(2)}, u32[]{:S(2)}) async-start(f32[64,1,256]{2,1,0:T(1,128)} %broadcast_in_dim.35), calls=%async_computation.3 | async-start | bytes 131072 | tf_op jit(solution)/shard_map/all_to_all | solution.py:38
Sparse Core Ops, SparseCore 0:
  107.0 37.6 all-gather.2
where the time goes:
time: 155 us; the launch traced here: 154 us
  starting transfers between devices  51.6 us (33%)
  waiting for transfers between devices  34.6 us (22%)
  matrix products  27.1 us (17%)
  local copies, waits for them, and re-layouts  15.6 us (10%)
  between operations  15.1 us (10%)
  other arithmetic  9.7 us (6%)
    all_to_all x4, starting transfers between devices, sent_to_all(): lax.all_to_all(jnp.broadcast_to(value[None], (devices, *value.shape)), ax...  27.4 us
    all_to_all x4, waiting for transfers between devices, sent_to_all(): lax.all_to_all(jnp.broadcast_to(value[None], (devices, *value.shape)), ax...  18.6 us
    dot_general x27, matrix products, per_device(): jnp.dot(window, conv_weight[time_off, row_off, col_off], preferred_elemen...  13.8 us
    all_gather x1, waiting for transfers between devices, total_of_pieces(): return lax.all_gather(value, axis).sum(0)  10.6 us
    ppermute x2, starting transfers between devices, padded_2(): lax.ppermute(lax.slice_in_dim(block, block.shape[dim] - width, None, axis...  7.52 us
    dot_general x27, matrix products, per_device(): lax.dot_general(grad_flat, window, (((0,), (0,)), ((), ())), preferred_el...  7.28 us
    all_to_all x1, starting transfers between devices, sent_and_summed(): lax.all_to_all(parts, axis, split_axis=0, concat_axis=0, tiled=True)  7.11 us
    ppermute x2, starting transfers between devices, from_behind(): return lax.ppermute(block, axis, route)  6.97 us
  transfers between devices with their start and end apart: 12, of which 5 were waited for; matrix products, arithmetic and copies ran while one was open for 31% of the time, Pallas kernels for 0%

commit v1 on v0

v1 whole, which is shorter than its diff:
```python
import functools
import math

import jax
import jax.numpy as jnp
from jax import lax
from jax.experimental import pallas as pl
from jax.experimental.pallas import tpu as pltpu
from jax.sharding import Mesh
from jax.sharding import PartitionSpec as P

G = 32
EPSILON = 1e-06
TM = ("z", "c")
ROWS = ("y", "x")
MESH = pl.DeviceIdType.MESH
WP = 128
HALF = 14
CHUNKS = 2
PER = HALF // CHUNKS
F32 = jnp.float32
BF16 = jnp.bfloat16


def group_total(per_channel, size):
    lanes = lax.broadcasted_iota(jnp.int32, per_channel.shape, 1)
    within = lanes % size
    channels = per_channel.shape[1]
    total = per_channel
    for step in range(1, size):
        ahead = pltpu.roll(per_channel, channels - step, 1)
        behind = pltpu.roll(per_channel, step, 1)
        total = total + jnp.where(within + step < size, ahead, 0.0)
        total = total + jnp.where(within >= step, behind, 0.0)
    return total


def kernel(
    sizes, x_hbm, gain_ref, bias_ref, w_hbm, cot_hbm,
    of_hbm, ig_hbm, wg_hbm, gain_hbm, bias_hbm,
    xr, cr, wv, a0, a3, c3, ct, ga, wgf, dsend, drecv, bsend, brecv, crecv, fin,
    ofv, igv, wgv, gv, bv, st1, st2, gs1, gs2,
    load_sem, out_sem, xs, xq, cs, cq, s1s, s1r, s2s, s2r, g1s, g1r, g2s, g2r,
    ds, dr, bs, br, zs, zr, fs, fr,
):
    nz, nc, ny, nx = sizes
    n_tm, n_rows = nz * nc, ny * nx
    frames, band, width, chans = x_hbm.shape
    pixels = frames * band * WP
    own_o = chans // n_rows
    all_pixels = frames * n_tm * band * n_rows * width
    cells = all_pixels * (chans // G)
    z, c = lax.axis_index("z"), lax.axis_index("c")
    y, x = lax.axis_index("y"), lax.axis_index("x")
    tm, row = z * nc + c, y * nx + x

    def at(t, r):
        t, r = lax.rem(t + n_tm, n_tm), lax.rem(r + n_rows, n_rows)
        return {"z": t // nc, "c": lax.rem(t, nc), "y": r // nx, "x": lax.rem(r, nx)}

    def xy_peers():
        for k in range(1, n_rows):
            dy, dx = k // nx, k % nx
            ty, tx = lax.rem(y + dy, ny), lax.rem(x + dx, nx)
            yield k, ty * nx + tx, {"z": z, "c": c, "y": ty, "x": tx}

    def zc_peers():
        for k in range(1, n_tm):
            dz, dc = k // nc, k % nc
            tz, tc = lax.rem(z + dz, nz), lax.rem(c + dc, nc)
            yield k, tz * nc + tc, {"z": tz, "c": tc, "y": y, "x": x}

    def remote(src, dst, send_sem, recv_sem, device):
        return pltpu.make_async_remote_copy(
            src_ref=src, dst_ref=dst, send_sem=send_sem, recv_sem=recv_sem,
            device_id=device, device_id_type=MESH,
        )

    load_x = pltpu.make_async_copy(x_hbm, xr.at[frames : 2 * frames, 1 : band + 1], load_sem.at[0])
    load_c = pltpu.make_async_copy(cot_hbm, cr.at[0:frames, 1 : band + 1], load_sem.at[1])
    load_w = pltpu.make_async_copy(w_hbm, wv, load_sem.at[2])
    load_x.start()
    load_c.start()
    load_w.start()

    barrier = pltpu.get_barrier_semaphore()
    partners = 0
    for _, _, device in (*zc_peers(), *xy_peers()):
        pl.semaphore_signal(barrier, inc=1, device_id=device, device_id_type=MESH)
        partners += 1
    for dt in (-1, 1):
        for dr_ in (-1, 1):
            pl.semaphore_signal(
                barrier, inc=1, device_id=at(tm + dt, row + dr_), device_id_type=MESH
            )
            partners += 1

    load_x.wait()

    def stat_row(k, carry):
        total, square = carry
        v = xr[frames + k // band, 1 + lax.rem(k, band)].astype(F32)
        return (
            total + v.reshape(width // 8, 8, chans).sum(axis=0),
            square + (v * v).reshape(width // 8, 8, chans).sum(axis=0),
        )

    zero8 = jnp.zeros((8, chans), F32)
    total, square = lax.fori_loop(0, frames * band, stat_row, (zero8, zero8))
    st1[row, 0:1] = total.sum(axis=0, keepdims=True)
    st1[row, 1:2] = square.sum(axis=0, keepdims=True)

    pl.semaphore_wait(barrier, partners)

    def spread_xy(slots, send_sem, recv_sem):
        return [
            remote(slots.at[row], slots.at[row], send_sem.at[k], recv_sem.at[row], device)
            for k, _, device in xy_peers()
        ]

    def spread_zc(slots, send_sem, recv_sem):
        return [
            remote(slots.at[tm], slots.at[tm], send_sem.at[k], recv_sem.at[tm], device)
            for k, _, device in zc_peers()
        ]

    def arrived_xy(slots, send_sem, recv_sem):
        for k, peer, device in xy_peers():
            remote(slots.at[peer], slots.at[peer], send_sem.at[k], recv_sem.at[peer], device).wait_recv()

    def arrived_zc(slots, send_sem, recv_sem):
        for k, peer, device in zc_peers():
            remote(slots.at[peer], slots.at[peer], send_sem.at[k], recv_sem.at[peer], device).wait_recv()

    def summed(slots):
        total = slots[0]
        for k in range(1, slots.shape[0]):
            total = total + slots[k]
        return total

    sent = spread_xy(st1, s1s, s1r)
    for copy in sent:
        copy.start()

    def margins(buf, first, there, way, send_sem, recv_sem):
        mine = buf.at[first : first + frames, 1 : band + 1]
        low = buf.at[first : first + frames, 1]
        high = buf.at[first : first + frames, band]
        same = buf.at[first : first + frames]
        moved = buf.at[there : there + frames]
        up_t = (tm + way >= 0) & (tm + way < n_tm)
        from_t = (tm - way >= 0) & (tm - way < n_tm)
        up_r, down_r = row < n_rows - 1, row > 0
        plan = [
            (high, same.at[:, 0], at(tm, row + 1), up_r, down_r),
            (low, same.at[:, band + 1], at(tm, row - 1), down_r, up_r),
            (mine, moved.at[:, 1 : band + 1], at(tm + way, row), up_t, from_t),
            (high, moved.at[:, 0], at(tm + way, row + 1), up_t & up_r, from_t & down_r),
            (low, moved.at[:, band + 1], at(tm + way, row - 1), up_t & down_r, from_t & up_r),
        ]
        return [
            (remote(src, dst, send_sem.at[k], recv_sem.at[k], device), sends, gets)
            for k, (src, dst, device, sends, gets) in enumerate(plan)
        ]

    load_c.wait()
    cot_margins = margins(cr, 0, frames, -1, cs, cq)
    x_margins = margins(xr, frames, 0, 1, xs, xq)
    for copy, sends, _ in (*cot_margins, *x_margins):

        @pl.when(sends)
        def _():
            copy.start()

    zeros_pad = jnp.zeros((WP - width, chans), F32)

    def padded_row(v):
        return jnp.concatenate([v, zeros_pad], axis=0)

    def cot_row(t, h, keep):
        v = padded_row(cr[t, h].astype(F32))
        v = jnp.where(keep, v, 0.0)
        sides = (pltpu.roll(v, 1, 0), v, pltpu.roll(v, WP - 1, 0))
        for shift in range(3):
            c3[shift, t, h] = sides[shift].astype(BF16)
        return sides

    for k in range(frames * band):
        sides = cot_row(k // band, 1 + k % band, True)
        for shift in range(3):
            ct[shift * chans : (shift + 1) * chans, k * WP : (k + 1) * WP] = (
                sides[2 - shift].T.astype(BF16)
            )
    load_w.wait()

    arrived_xy(st1, s1s, s1r)
    st2[tm] = summed(st1)
    sent2 = spread_zc(st2, s2s, s2r)
    for copy in sent2:
        copy.start()

    for copy, _, gets in cot_margins:

        @pl.when(gets)
        def _():
            copy.wait_recv()

    row_low, row_high = row > 0, row < n_rows - 1

    def cot_margin_row(t, h):
        keep = True
        if t >= frames:
            keep = tm < n_tm - 1
        if h == 0:
            keep = keep & row_low
        if h == band + 1:
            keep = keep & row_high
        cot_row(t, h, keep)

    for t in range(2 * frames):
        for h in range(band + 2):
            if not (t < frames and 1 <= h <= band):
                cot_margin_row(t, h)

    def window(ref, a, b):
        return ref[pl.ds(a, frames), b : b + band].reshape(pixels, chans)

    taps = [(b, s) for b in range(3) for s in range(3)]
    for a in range(3):
        lhs = jnp.concatenate([window(c3.at[s], a, b) for b, s in taps], axis=1)
        rhs = jnp.concatenate([wv[9 * (2 - a) + 3 * (2 - b) + 2 - s] for b, s in taps], axis=1)
        part = lax.dot_general(lhs, rhs, (((1,), (1,)), ((), ())), preferred_element_type=F32)
        if a == 0:
            ga[...] = part
        else:
            ga[...] += part

    arrived_zc(st2, s2s, s2r)
    stats = summed(st2)
    wide = lambda v: jnp.broadcast_to(v, (8, chans))
    mean = group_total(wide(stats[0:1]), chans // G) / cells
    variance = group_total(wide(stats[1:2]), chans // G) / cells - mean * mean
    inverse = lax.rsqrt(variance + EPSILON)
    gain, shift_ = wide(gain_ref[...]), wide(bias_ref[...])
    mean, inverse, gain, shift_ = (v[0:1] for v in (mean, inverse, gain, shift_))

    for copy, _, gets in x_margins:

        @pl.when(gets)
        def _():
            copy.wait_recv()

    def act_row(k, carry):
        t, h = k // (band + 2), lax.rem(k, band + 2)
        v = xr[t, h].astype(F32)
        pre = (v - mean) * inverse * gain + shift_
        keep = (
            ((t >= frames) | (tm > 0))
            & ((h >= 1) | row_low)
            & ((h <= band) | row_high)
        )
        act = jnp.where(keep, pre / (1.0 + jnp.exp(-pre)), 0.0)
        a0[t, h] = padded_row(act).astype(BF16)
        return carry

    lax.fori_loop(0, 2 * frames * (band + 2), act_row, 0)

    first = c == 0
    other = {"z": z, "c": 1 - c, "y": y, "x": x}
    part0 = jnp.where(first, 5, 0)
    part1 = jnp.where(first, 0, 9)
    halves = (
        remote(dsend.at[pl.ds(part0, 9)], drecv.at[pl.ds(part0, 9)], ds.at[0], dr.at[0], other),
        remote(dsend.at[pl.ds(part1, 5)], drecv.at[pl.ds(part1, 5)], ds.at[1], dr.at[1], other),
    )
    got0, got1 = jnp.where(first, 0, 5), jnp.where(first, 9, 0)
    halves_in = (
        remote(dsend.at[pl.ds(got0, 9)], drecv.at[pl.ds(got0, 9)], ds.at[0], dr.at[0], other),
        remote(dsend.at[pl.ds(got1, 5)], drecv.at[pl.ds(got1, 5)], ds.at[1], dr.at[1], other),
    )
    for k in range(3):
        a = jnp.where(first, 2 - k, k)
        rhs = jnp.concatenate([window(a0, a, b) for b in range(3)], axis=1)
        part = jnp.dot(ct[...], rhs, preferred_element_type=F32)
        for b in range(3):
            for s in range(3):
                block = part[s * chans : (s + 1) * chans, b * chans : (b + 1) * chans]
                if k == 0:
                    dsend[part0 + 3 * b + s] = block.astype(BF16)
                else:
                    wgf[9 * a + 3 * b + s] = block
        if k == 0:
            halves[0].start()
        if k == 1:
            at1 = jnp.where(first, 13, 9)
            for j in range(5):
                dsend[part1 + j] = wgf[at1 + j].astype(BF16)
            halves[1].start()

    for copy in halves_in:
        copy.wait_recv()
    base = jnp.where(first, 0, 13)
    to_rows = []
    for ch in range(CHUNKS):
        for j in range(PER):
            value = wgf[base + ch * PER + j] + drecv[ch * PER + j].astype(F32)
            bsend[ch, :, j] = value.reshape(n_rows, own_o, chans).astype(BF16)
        brecv[ch, row] = bsend[ch, row]
        for k, peer, device in xy_peers():
            copy = remote(
                bsend.at[ch, peer], brecv.at[ch, row], bs.at[ch, k], br.at[ch, row], device
            )
            copy.start()
            to_rows.append(copy)

    def pre_row(k):
        v = xr[frames + k // band, 1 + lax.rem(k, band)].astype(F32)
        normed = (v - mean) * inverse
        return normed

    def grad_row(k, carry):
        gains, biases = carry
        normed = pre_row(k)
        pre = normed * gain + shift_
        sig = 1.0 / (1.0 + jnp.exp(-pre))
        at_k = pl.multiple_of(k * WP, WP)
        grad = ga[pl.ds(at_k, width)] * sig * (1.0 + pre * (1.0 - sig))
        ga[pl.ds(at_k, width)] = grad
        return (
            gains + (grad * normed).reshape(width // 8, 8, chans).sum(axis=0),
            biases + grad.reshape(width // 8, 8, chans).sum(axis=0),
        )

    gains, biases = lax.fori_loop(0, frames * band, grad_row, (zero8, zero8))
    gs1[row, 0:1] = gains.sum(axis=0, keepdims=True)
    gs1[row, 1:2] = biases.sum(axis=0, keepdims=True)
    sent3 = spread_xy(gs1, g1s, g1r)
    for copy in sent3:
        copy.start()

    def shift_row(k, carry):
        t, h = k // (band + 2), lax.rem(k, band + 2)
        v = a0[t, h].astype(F32)
        a3[0, t, h] = pltpu.roll(v, 1, 0).astype(BF16)
        a3[1, t, h] = pltpu.roll(v, WP - 1, 0).astype(BF16)
        return carry

    lax.fori_loop(0, 2 * frames * (band + 2), shift_row, 0)
    sides = (a3.at[0], a0, a3.at[1])
    conv = None
    for a in range(3):
        lhs = jnp.concatenate([window(sides[s], a, b) for b, s in taps], axis=1)
        rhs = jnp.concatenate([wv[9 * a + 3 * b + s] for b, s in taps], axis=0)
        part = jnp.dot(lhs, rhs, preferred_element_type=F32)
        conv = part if a == 0 else conv + part
    conv = conv.reshape(frames, band, WP, chans)
    for t in range(frames):
        for h in range(band):
            v = xr[frames + t, 1 + h].astype(F32)
            ofv[t, h] = (v + conv[t, h, :width]).astype(BF16)
    put_of = pltpu.make_async_copy(ofv, of_hbm, out_sem.at[0])
    put_of.start()

    arrived_xy(gs1, g1s, g1r)
    gs2[tm] = summed(gs1)
    sent4 = spread_zc(gs2, g2s, g2r)
    for copy in sent4:
        copy.start()

    to_z = []
    for ch in range(CHUNKS):
        for k, peer, device in xy_peers():
            remote(
                bsend.at[ch, peer], brecv.at[ch, peer], bs.at[ch, k], br.at[ch, peer], device
            ).wait_recv()
        value = brecv[ch, 0].astype(F32)
        for k in range(1, n_rows):
            value = value + brecv[ch, k].astype(F32)
        crecv[ch, z] = value.astype(BF16)
        for k in range(1, nz):
            device = {"z": lax.rem(z + k, nz), "c": c, "y": y, "x": x}
            copy = remote(crecv.at[ch, z], crecv.at[ch, z], zs.at[ch, k], zr.at[ch, z], device)
            copy.start()
            to_z.append(copy)

    arrived_zc(gs2, g2s, g2r)
    sums = summed(gs2)
    gain_grad, bias_grad = wide(sums[0:1]), wide(sums[1:2])
    gv[...] = sums[0:1]
    bv[...] = sums[1:2]
    put_g = pltpu.make_async_copy(gv, gain_hbm, out_sem.at[3])
    put_b = pltpu.make_async_copy(bv, bias_hbm, out_sem.at[4])
    put_g.start()
    put_b.start()
    mean_dn = (group_total(gain * bias_grad, chans // G) / cells)[0:1]
    mean_dnn = (group_total(gain * gain_grad, chans // G) / cells)[0:1]

    def input_row(k, carry):
        t, h = k // band, lax.rem(k, band)
        normed = pre_row(k)
        grad = ga[pl.ds(pl.multiple_of(k * WP, WP), width)]
        cot = cr[t, 1 + h].astype(F32)
        igv[t, h] = (inverse * (grad * gain - mean_dn - normed * mean_dnn) + cot).astype(BF16)
        return carry

    lax.fori_loop(0, frames * band, input_row, 0)
    put_ig = pltpu.make_async_copy(igv, ig_hbm, out_sem.at[1])
    put_ig.start()

    to_core = []
    for ch in range(CHUNKS):
        for k in range(1, nz):
            peer = lax.rem(z + k, nz)
            device = {"z": peer, "c": c, "y": y, "x": x}
            remote(
                crecv.at[ch, peer], crecv.at[ch, peer], zs.at[ch, k], zr.at[ch, peer], device
            ).wait_recv()
        value = crecv[ch, 0].astype(F32)
        for k in range(1, nz):
            value = value + crecv[ch, k].astype(F32)
        fin[c, ch] = value
        copy = remote(fin.at[c, ch], fin.at[c, ch], fs.at[ch], fr.at[ch], other)
        copy.start()
        to_core.append(copy)
    for ch in range(CHUNKS):
        remote(fin.at[1 - c, ch], fin.at[1 - c, ch], fs.at[ch], fr.at[ch], other).wait_recv()
    scale = 1.0 / math.sqrt(all_pixels)
    for j in range(27):
        if j < HALF:
            value = fin[0, j // PER, j % PER]
        else:
            value = fin[1, (j - 13) // PER, (j - 13) % PER]
        wgv[:, j * chans : (j + 1) * chans] = value * scale
    put_wg = pltpu.make_async_copy(wgv, wg_hbm, out_sem.at[2])
    put_wg.start()

    for copy in (*sent, *sent2, *sent3, *sent4, *halves, *to_rows, *to_z, *to_core):
        copy.wait_send()
    for copy, sends, _ in (*cot_margins, *x_margins):

        @pl.when(sends)
        def _():
            copy.wait_send()

    for copy in (put_of, put_ig, put_g, put_b, put_wg):
        copy.wait()


def per_device(sizes, frames_in, norm_gain, norm_bias, conv_weight, cotangent):
    nz, nc, ny, nx = sizes
    n_tm, n_rows = nz * nc, ny * nx
    frames, band, width, chans = frames_in.shape
    own_o = chans // n_rows
    rows = (2 * frames, band + 2)
    vmem, dma = pltpu.VMEM, pltpu.SemaphoreType.DMA
    scratch = [
        vmem((*rows, width, chans), BF16),
        vmem((*rows, width, chans), BF16),
        vmem((27, chans, chans), BF16),
        vmem((*rows, WP, chans), BF16),
        vmem((2, *rows, WP, chans), BF16),
        vmem((3, *rows, WP, chans), BF16),
        vmem((3 * chans, frames * band * WP), BF16),
        vmem((frames * band * WP, chans), F32),
        vmem((27, chans, chans), F32),
        vmem((HALF, chans, chans), BF16),
        vmem((HALF, chans, chans), BF16),
        vmem((CHUNKS, n_rows, PER, own_o, chans), BF16),
        vmem((CHUNKS, n_rows, PER, own_o, chans), BF16),
        vmem((CHUNKS, nz, PER, own_o, chans), BF16),
        vmem((2, CHUNKS, PER, own_o, chans), F32),
        vmem((frames, band, width, chans), BF16),
        vmem((frames, band, width, chans), BF16),
        vmem((own_o, 27 * chans), F32),
        vmem((1, chans), F32),
        vmem((1, chans), F32),
        vmem((n_rows, 2, chans), F32),
        vmem((n_tm, 2, chans), F32),
        vmem((n_rows, 2, chans), F32),
        vmem((n_tm, 2, chans), F32),
        dma((3,)), dma((5,)),
        dma((5,)), dma((5,)), dma((5,)), dma((5,)),
        dma((n_rows,)), dma((n_rows,)), dma((n_tm,)), dma((n_tm,)),
        dma((n_rows,)), dma((n_rows,)), dma((n_tm,)), dma((n_tm,)),
        dma((2,)), dma((2,)),
        dma((CHUNKS, n_rows)), dma((CHUNKS, n_rows)),
        dma((CHUNKS, nz)), dma((CHUNKS, nz)),
        dma((CHUNKS,)), dma((CHUNKS,)),
    ]
    anywhere = pl.BlockSpec(memory_space=pl.ANY)
    inside = pl.BlockSpec(memory_space=pltpu.VMEM)
    out = jax.ShapeDtypeStruct
    of, ig, wg, gg, bg = pl.pallas_call(
        functools.partial(kernel, sizes),
        out_shape=(
            out(frames_in.shape, BF16),
            out(frames_in.shape, BF16),
            out((own_o, 27 * chans), F32),
            out((1, chans), F32),
            out((1, chans), F32),
        ),
        in_specs=[anywhere, inside, inside, anywhere, anywhere],
        out_specs=(anywhere,) * 5,
        scratch_shapes=scratch,
        compiler_params=pltpu.CompilerParams(
            collective_id=0, has_side_effects=True, vmem_limit_bytes=48 << 20
        ),
        name="block",
    )(
        frames_in,
        norm_gain.reshape(1, chans),
        norm_bias.reshape(1, chans),
        conv_weight.reshape(27, chans, chans),
        cotangent,
    )
    return of, ig, wg, gg.reshape(chans), bg.reshape(chans)


def program(devices):
    torus = Mesh(devices, ("z", "c", "y", "x"))
    placed = (P(TM, ROWS, None, None), P(), P(), P(), P(TM, ROWS, None, None))
    return jax.shard_map(
        functools.partial(per_device, devices.shape),
        mesh=torus,
        in_specs=placed,
        out_specs=(P(TM, ROWS, None, None), P(TM, ROWS, None, None), P(ROWS, None), P(), P()),
        check_vma=False,
    )


def solution(mesh):
    return program(mesh.devices.reshape(8, 2, 4, 4))
```

time: 155 us -> 53.3 us (0.34)
  starting transfers between devices: 51.6 us -> 0 us
  Pallas kernels: 0 us -> 45.7 us
  waiting for transfers between devices: 34.6 us -> 0 us
  matrix products: 27.1 us -> 0 us
  between operations: 15.1 us -> 0.66 us
  other arithmetic: 9.7 us -> 0 us
  local copies, waits for them, and re-layouts: 15.6 us -> 6.76 us
    pallas_call x0 -> x1, Pallas kernels: none -> 45.7 us  [per_device(): pl.pallas_call(functools.partial(kernel, sizes), out_shape=(out(frames_in...]
    all_to_all x5 -> x0, starting transfers between devices: 34.5 us -> none  [the longest x4 27.4 us: sent_to_all(): lax.all_to_all(jnp.broadcast_to(value[None], (devices, *value.shape)), ax...]
    dot_general x81 -> x0, matrix products: 27.1 us -> none  [the longest x27 13.8 us: per_device(): jnp.dot(window, conv_weight[time_off, row_off, col_off], preferred_elemen...]
    all_to_all x5 -> x0, waiting for transfers between devices: 24 us -> none  [the longest x4 18.6 us: sent_to_all(): lax.all_to_all(jnp.broadcast_to(value[None], (devices, *value.shape)), ax...]
    ppermute x6 -> x0, starting transfers between devices: 17.1 us -> none  [the longest x2 7.52 us: padded_2(): lax.ppermute(lax.slice_in_dim(block, block.shape[dim] - width, None, axis...]
    all_gather x1 -> x0, waiting for transfers between devices: 10.6 us -> none  [total_of_pieces(): return lax.all_gather(value, axis).sum(0)]
    slice x6 -> x0, local copies, waits for them, and re-layouts: 5.49 us -> none  [the longest x3 4.17 us: per_device(): padded[time_off:time_off + frames, row_off:row_off + band_rows, col_off:c...]
    reduce_sum x12 -> x0, other arithmetic: 4.32 us -> none  [the longest x1 1.57 us: total_of_pieces(): return lax.all_gather(value, axis).sum(0)]
  transfers between devices with their start and end apart: 12 -> 0, of which waited for: 5 -> 0; matrix products, arithmetic and copies ran while one was open for 31% -> 0% of each run, Pallas kernels for 0% -> 0%
where the time goes in v1:
time: 53.3 us; the launch traced here: 53.1 us
  Pallas kernels  45.7 us (86%)
  local copies, waits for them, and re-layouts  6.76 us (13%)
  between operations  0.66 us (1%)
    pallas_call x1, Pallas kernels, per_device(): pl.pallas_call(functools.partial(kernel, sizes), out_shape=(out(frames_in...  45.7 us
    unnamed x15, local copies, waits for them, and re-layouts  6.76 us

profile of v1, /device:TPU:1, one launch (start us, length us, event | category | flops | bytes accessed | tf_op | source)
XLA Modules:
  0.0 53.1 jit_solution(11704302763155602387)
XLA Ops:
  0.6 0.0 copy-start.3
  0.6 0.0 copy-start.4
  0.7 0.6 %copy-done.3 = f32[128]{0:T(128)S(1)} copy-done((f32[128]{0:T(128)S(1)}, f32[128]{0:T(128)}, u32[]{:S(2)}) %copy-start.3) | copy-done | bytes 536
  1.3 0.0 copy-done.4
  1.3 0.0 copy-start
  1.3 1.2 %copy-done = bf16[3,3,3,128,128]{4,3,2,1,0:T(8,128)(2,1)S(1)} copy-done((bf16[3,3,3,128,128]{4,3,2,1,0:T(8,128)(2,1)S(1)}, bf16[3,3,3,128,128]{4,3,2,1,0:T(8,128)(2,1)}, u32[]{:S(2)}) %copy-start) | copy-done | bytes 884760
  2.5 0.0 copy-start.1
  2.5 0.9 %copy-done.1 = bf16[2,4,120,128]{3,2,1,0:T(8,128)(2,1)S(1)} copy-done((bf16[2,4,120,128]{3,2,1,0:T(8,128)(2,1)S(1)}, bf16[2,4,120,128]{3,2,1,0:T(8,128)(2,1)}, u32[]{:S(2)}) %copy-start.1) | copy-done | bytes 245784
  3.4 0.0 copy-start.2
  3.4 0.9 %copy-done.2 = bf16[2,4,120,128]{3,2,1,0:T(8,128)(2,1)S(1)} copy-done((bf16[2,4,120,128]{3,2,1,0:T(8,128)(2,1)S(1)}, bf16[2,4,120,128]{3,2,1,0:T(8,128)(2,1)}, u32[]{:S(2)}) %copy-start.2) | copy-done | bytes 245784
  4.4 45.7 %block.1 = (bf16[2,4,120,128]{3,2,1,0:T(8,128)(2,1)S(1)}, bf16[2,4,120,128]{3,2,1,0:T(8,128)(2,1)S(1)}, f32[8,3456]{1,0:T(8,128)S(1)}, f32[1,128]{1,0:T(1,128)S(1)}, f32[1,128]{1,0:T(1,128)S(1)}) custom-call(bf16[2,4,120,128]{3,2,1,0:T(8,128)(2,1)S(1)} %copy-done.1, f32[1,128]{1,0:T(1,128)S(1)} %bitcast.6, f32[1,128]{1,0:T(1,128)S(1)} %bitcast.7, ...), custom_call_target="tpu_custom_call" | custom-call | tf_op jit(solution)/shard_map/block/pallas_call | solution.py:493
  50.0 0.7 %copy.15 = bf16[2,4,120,128]{3,2,1,0:T(8,128)(2,1)} copy(bf16[2,4,120,128]{3,2,1,0:T(8,128)(2,1)S(1)} %get-tuple-element.20) | data formatting | bytes 491520
  50.7 0.7 %copy.16 = bf16[2,4,120,128]{3,2,1,0:T(8,128)(2,1)} copy(bf16[2,4,120,128]{3,2,1,0:T(8,128)(2,1)S(1)} %get-tuple-element.21) | data formatting | bytes 491520
  51.4 0.6 %copy.17 = f32[8,3456]{1,0:T(8,128)} copy(f32[8,3456]{1,0:T(8,128)S(1)} %get-tuple-element.22) | data formatting | bytes 221184
  52.1 0.5 copy.18
  52.6 0.5 copy.19
Async XLA Ops:
  0.6 0.7 %copy-start.3 = (f32[128]{0:T(128)S(1)}, f32[128]{0:T(128)}, u32[]{:S(2)}) copy-start(f32[128]{0:T(128)} %param.6) | copy-start | bytes 1540
  0.6 0.7 %copy-start.4 = (f32[128]{0:T(128)S(1)}, f32[128]{0:T(128)}, u32[]{:S(2)}) copy-start(f32[128]{0:T(128)} %param.7) | copy-start | bytes 1540
  1.3 1.2 %copy-start = (bf16[3,3,3,128,128]{4,3,2,1,0:T(8,128)(2,1)S(1)}, bf16[3,3,3,128,128]{4,3,2,1,0:T(8,128)(2,1)}, u32[]{:S(2)}) copy-start(bf16[3,3,3,128,128]{4,3,2,1,0:T(8,128)(2,1)} %param.8) | copy-start | bytes 2654212
  2.5 0.9 %copy-start.1 = (bf16[2,4,120,128]{3,2,1,0:T(8,128)(2,1)S(1)}, bf16[2,4,120,128]{3,2,1,0:T(8,128)(2,1)}, u32[]{:S(2)}) copy-start(bf16[2,4,120,128]{3,2,1,0:T(8,128)(2,1)} %x_hbm.1) | copy-start | bytes 737284
  3.4 0.9 %copy-start.2 = (bf16[2,4,120,128]{3,2,1,0:T(8,128)(2,1)S(1)}, bf16[2,4,120,128]{3,2,1,0:T(8,128)(2,1)}, u32[]{:S(2)}) copy-start(bf16[2,4,120,128]{3,2,1,0:T(8,128)(2,1)} %cot_hbm.1) | copy-start | bytes 737284

commit v2 on v1

--- a/solution.py
+++ b/solution.py
@@ -15,9 +15,8 @@
 ROWS = ("y", "x")
 MESH = pl.DeviceIdType.MESH
 WP = 128
-HALF = 14
-CHUNKS = 2
-PER = HALF // CHUNKS
+CHUNKS = 3
+PER = 5
 F32 = jnp.float32
 BF16 = jnp.bfloat16
 
@@ -36,9 +35,9 @@
 
 
 def kernel(
-    sizes, x_hbm, gain_ref, bias_ref, w_hbm, cot_hbm,
+    sizes, x_hbm, gn_hbm, sh_hbm, w_hbm, cot_hbm,
     of_hbm, ig_hbm, wg_hbm, gain_hbm, bias_hbm,
-    xr, cr, wv, a0, a3, c3, ct, ga, wgf, dsend, drecv, bsend, brecv, crecv, fin,
+    gain_ref, bias_ref, xr, cr, wv, a0, a3, c3, ct, ga, wgf, dsend, drecv, bsend, brecv, crecv, fin,
     ofv, igv, wgv, gv, bv, st1, st2, gs1, gs2,
     load_sem, out_sem, xs, xq, cs, cq, s1s, s1r, s2s, s2r, g1s, g1r, g2s, g2r,
     ds, dr, bs, br, zs, zr, fs, fr,
@@ -79,9 +78,10 @@
     load_x = pltpu.make_async_copy(x_hbm, xr.at[frames : 2 * frames, 1 : band + 1], load_sem.at[0])
     load_c = pltpu.make_async_copy(cot_hbm, cr.at[0:frames, 1 : band + 1], load_sem.at[1])
     load_w = pltpu.make_async_copy(w_hbm, wv, load_sem.at[2])
-    load_x.start()
-    load_c.start()
-    load_w.start()
+    load_gn = pltpu.make_async_copy(gn_hbm, gain_ref, load_sem.at[3])
+    load_sh = pltpu.make_async_copy(sh_hbm, bias_ref, load_sem.at[4])
+    for copy in (load_x, load_c, load_w, load_gn, load_sh):
+        copy.start()
 
     barrier = pltpu.get_barrier_semaphore()
     partners = 0
@@ -192,6 +192,8 @@
                 sides[2 - shift].T.astype(BF16)
             )
     load_w.wait()
+    load_gn.wait()
+    load_sh.wait()
 
     arrived_xy(st1, s1s, s1r)
     st2[tm] = summed(st1)
@@ -199,41 +201,53 @@
     for copy in sent2:
         copy.start()
 
-    for copy, _, gets in cot_margins:
+    row_low, row_high = row > 0, row < n_rows - 1
+    for copy, _, gets in cot_margins[:2]:
 
         @pl.when(gets)
         def _():
             copy.wait_recv()
 
-    row_low, row_high = row > 0, row < n_rows - 1
-
-    def cot_margin_row(t, h):
-        keep = True
-        if t >= frames:
-            keep = tm < n_tm - 1
-        if h == 0:
-            keep = keep & row_low
-        if h == band + 1:
-            keep = keep & row_high
-        cot_row(t, h, keep)
-
-    for t in range(2 * frames):
+    for t in range(frames):
+        cot_row(t, 0, row_low)
+        cot_row(t, band + 1, row_high)
+
+    taps = [(b, s) for b in range(3) for s in range(3)]
+
+    def frame(refs, t):
+        rows = [refs[s][t, b : b + band].reshape(band * WP, chans) for b, s in taps]
+        return jnp.concatenate(rows, axis=1)
+
+    def back_taps(a):
+        return jnp.concatenate([wv[9 * (2 - a) + 3 * (2 - b) + 2 - s] for b, s in taps], axis=1)
+
+    def back(lhs, rhs):
+        return lax.dot_general(lhs, rhs, (((1,), (1,)), ((), ())), preferred_element_type=F32)
+
+    half = band * WP
+    c3s = [c3.at[s] for s in range(3)]
+    both = back(frame(c3s, 1), jnp.concatenate([back_taps(1), back_taps(0)], axis=0))
+    ga[0:half] = back(frame(c3s, 0), back_taps(0)) + both[:, :chans]
+    ga[half:] = both[:, chans:]
+
+    for copy, _, gets in cot_margins[2:]:
+
+        @pl.when(gets)
+        def _():
+            copy.wait_recv()
+
+    has_next = tm < n_tm - 1
+    for t in range(frames, 2 * frames):
         for h in range(band + 2):
-            if not (t < frames and 1 <= h <= band):
-                cot_margin_row(t, h)
-
-    def window(ref, a, b):
-        return ref[pl.ds(a, frames), b : b + band].reshape(pixels, chans)
-
-    taps = [(b, s) for b in range(3) for s in range(3)]
-    for a in range(3):
-        lhs = jnp.concatenate([window(c3.at[s], a, b) for b, s in taps], axis=1)
-        rhs = jnp.concatenate([wv[9 * (2 - a) + 3 * (2 - b) + 2 - s] for b, s in taps], axis=1)
-        part = lax.dot_general(lhs, rhs, (((1,), (1,)), ((), ())), preferred_element_type=F32)
-        if a == 0:
-            ga[...] = part
-        else:
-            ga[...] += part
+            keep = has_next
+            if h == 0:
+                keep = keep & row_low
+            if h == band + 1:
+                keep = keep & row_high
+            cot_row(t, h, keep)
+    both = back(frame(c3s, 2), jnp.concatenate([back_taps(2), back_taps(1)], axis=0))
+    ga[0:half] += both[:, :chans]
+    ga[half:] += back(frame(c3s, 3), back_taps(2)) + both[:, chans:]
 
     arrived_zc(st2, s2s, s2r)
     stats = summed(st2)
@@ -249,6 +263,9 @@
         @pl.when(gets)
         def _():
             copy.wait_recv()
+
+    def sigmoid(v):
+        return 0.5 + 0.5 * jnp.tanh(0.5 * v)
 
     def act_row(k, carry):
         t, h = k // (band + 2), lax.rem(k, band + 2)
@@ -259,70 +276,58 @@
             & ((h >= 1) | row_low)
             & ((h <= band) | row_high)
         )
-        act = jnp.where(keep, pre / (1.0 + jnp.exp(-pre)), 0.0)
-        a0[t, h] = padded_row(act).astype(BF16)
+        a0[t, h] = padded_row(jnp.where(keep, pre * sigmoid(pre), 0.0)).astype(BF16)
         return carry
 
-    lax.fori_loop(0, 2 * frames * (band + 2), act_row, 0)
-
-    first = c == 0
+    def act_frames(low, high):
+        lax.fori_loop(low * (band + 2), high * (band + 2), act_row, 0)
+
     other = {"z": z, "c": 1 - c, "y": y, "x": x}
-    part0 = jnp.where(first, 5, 0)
-    part1 = jnp.where(first, 0, 9)
-    halves = (
-        remote(dsend.at[pl.ds(part0, 9)], drecv.at[pl.ds(part0, 9)], ds.at[0], dr.at[0], other),
-        remote(dsend.at[pl.ds(part1, 5)], drecv.at[pl.ds(part1, 5)], ds.at[1], dr.at[1], other),
-    )
-    got0, got1 = jnp.where(first, 0, 5), jnp.where(first, 9, 0)
-    halves_in = (
-        remote(dsend.at[pl.ds(got0, 9)], drecv.at[pl.ds(got0, 9)], ds.at[0], dr.at[0], other),
-        remote(dsend.at[pl.ds(got1, 5)], drecv.at[pl.ds(got1, 5)], ds.at[1], dr.at[1], other),
-    )
-    for k in range(3):
-        a = jnp.where(first, 2 - k, k)
-        rhs = jnp.concatenate([window(a0, a, b) for b in range(3)], axis=1)
+    given, kept = 4 * (1 - c), 4 * c
+    halves = [
+        remote(dsend.at[a], drecv.at[a], ds.at[a], dr.at[a], other) for a in range(CHUNKS)
+    ]
+
+    def weight_blocks(a):
+        rhs = jnp.concatenate(
+            [a0[a : a + frames, b : b + band].reshape(pixels, chans) for b in range(3)], axis=1
+        )
         part = jnp.dot(ct[...], rhs, preferred_element_type=F32)
-        for b in range(3):
-            for s in range(3):
-                block = part[s * chans : (s + 1) * chans, b * chans : (b + 1) * chans]
-                if k == 0:
-                    dsend[part0 + 3 * b + s] = block.astype(BF16)
-                else:
-                    wgf[9 * a + 3 * b + s] = block
-        if k == 0:
-            halves[0].start()
-        if k == 1:
-            at1 = jnp.where(first, 13, 9)
-            for j in range(5):
-                dsend[part1 + j] = wgf[at1 + j].astype(BF16)
-            halves[1].start()
-
-    for copy in halves_in:
-        copy.wait_recv()
-    base = jnp.where(first, 0, 13)
+        for b, s in taps:
+            wgf[a, 3 * b + s] = part[s * chans : (s + 1) * chans, b * chans : (b + 1) * chans]
+        for j in range(PER):
+            dsend[a, j] = wgf[a, given + j].astype(BF16)
+        halves[a].start()
+
     to_rows = []
-    for ch in range(CHUNKS):
+
+    def send_rows(a):
+        halves[a].wait_recv()
         for j in range(PER):
-            value = wgf[base + ch * PER + j] + drecv[ch * PER + j].astype(F32)
-            bsend[ch, :, j] = value.reshape(n_rows, own_o, chans).astype(BF16)
-        brecv[ch, row] = bsend[ch, row]
+            value = wgf[a, kept + j] + drecv[a, j].astype(F32)
+            bsend[a, :, j] = value.reshape(n_rows, own_o, chans).astype(BF16)
+        brecv[a, row] = bsend[a, row]
         for k, peer, device in xy_peers():
             copy = remote(
-                bsend.at[ch, peer], brecv.at[ch, row], bs.at[ch, k], br.at[ch, row], device
+                bsend.at[a, peer], brecv.at[a, row], bs.at[a, k], br.at[a, row], device
             )
             copy.start()
             to_rows.append(copy)
 
+    act_frames(0, 2)
+    weight_blocks(0)
+    act_frames(2, 3)
+    weight_blocks(1)
+
     def pre_row(k):
         v = xr[frames + k // band, 1 + lax.rem(k, band)].astype(F32)
-        normed = (v - mean) * inverse
-        return normed
+        return (v - mean) * inverse
 
     def grad_row(k, carry):
         gains, biases = carry
         normed = pre_row(k)
         pre = normed * gain + shift_
-        sig = 1.0 / (1.0 + jnp.exp(-pre))
+        sig = sigmoid(pre)
         at_k = pl.multiple_of(k * WP, WP)
         grad = ga[pl.ds(at_k, width)] * sig * (1.0 + pre * (1.0 - sig))
         ga[pl.ds(at_k, width)] = grad
@@ -338,6 +343,12 @@
     for copy in sent3:
         copy.start()
 
+    send_rows(0)
+    act_frames(3, 4)
+    weight_blocks(2)
+    send_rows(1)
+    send_rows(2)
+
     def shift_row(k, carry):
         t, h = k // (band + 2), lax.rem(k, band + 2)
         v = a0[t, h].astype(F32)
@@ -347,17 +358,22 @@
 
     lax.fori_loop(0, 2 * frames * (band + 2), shift_row, 0)
     sides = (a3.at[0], a0, a3.at[1])
-    conv = None
-    for a in range(3):
-        lhs = jnp.concatenate([window(sides[s], a, b) for b, s in taps], axis=1)
-        rhs = jnp.concatenate([wv[9 * a + 3 * b + s] for b, s in taps], axis=0)
-        part = jnp.dot(lhs, rhs, preferred_element_type=F32)
-        conv = part if a == 0 else conv + part
-    conv = conv.reshape(frames, band, WP, chans)
-    for t in range(frames):
+
+    def front_taps(a):
+        return jnp.concatenate([wv[9 * a + 3 * b + s] for b, s in taps], axis=0)
+
+    def front(lhs, rhs):
+        return jnp.dot(lhs, rhs, preferred_element_type=F32)
+
+    def put_frame(t, conv):
         for h in range(band):
             v = xr[frames + t, 1 + h].astype(F32)
-            ofv[t, h] = (v + conv[t, h, :width]).astype(BF16)
+            ofv[t, h] = (v + conv[h * WP : h * WP + width]).astype(BF16)
+
+    one = front(frame(sides, 1), jnp.concatenate([front_taps(1), front_taps(0)], axis=1))
+    two = front(frame(sides, 2), jnp.concatenate([front_taps(2), front_taps(1)], axis=1))
+    put_frame(0, front(frame(sides, 0), front_taps(0)) + one[:, :chans] + two[:, :chans])
+    put_frame(1, front(frame(sides, 3), front_taps(2)) + one[:, chans:] + two[:, chans:])
     put_of = pltpu.make_async_copy(ofv, of_hbm, out_sem.at[0])
     put_of.start()
 
@@ -426,10 +442,8 @@
         remote(fin.at[1 - c, ch], fin.at[1 - c, ch], fs.at[ch], fr.at[ch], other).wait_recv()
     scale = 1.0 / math.sqrt(all_pixels)
     for j in range(27):
-        if j < HALF:
-            value = fin[0, j // PER, j % PER]
-        else:
-            value = fin[1, (j - 13) // PER, (j - 13) % PER]
+        a, m = j // 9, j % 9
+        value = fin[0, a, m] if m < PER else fin[1, a, m - 4]
         wgv[:, j * chans : (j + 1) * chans] = value * scale
     put_wg = pltpu.make_async_copy(wgv, wg_hbm, out_sem.at[2])
     put_wg.start()
@@ -443,6 +457,15 @@
             copy.wait_send()
 
     for copy in (put_of, put_ig, put_g, put_b, put_wg):
+        copy.wait()
+
+
+def put_out(*refs):
+    sources, places, sem = refs[:5], refs[5:10], refs[10]
+    copies = [pltpu.make_async_copy(s, d, sem.at[k]) for k, (s, d) in enumerate(zip(sources, places))]
+    for copy in copies:
+        copy.start()
+    for copy in copies:
         copy.wait()
 
 
@@ -454,6 +477,8 @@
     rows = (2 * frames, band + 2)
     vmem, dma = pltpu.VMEM, pltpu.SemaphoreType.DMA
     scratch = [
+        vmem((1, chans), F32),
+        vmem((1, chans), F32),
         vmem((*rows, width, chans), BF16),
         vmem((*rows, width, chans), BF16),
         vmem((27, chans, chans), BF16),
@@ -462,9 +487,9 @@
         vmem((3, *rows, WP, chans), BF16),
         vmem((3 * chans, frames * band * WP), BF16),
         vmem((frames * band * WP, chans), F32),
-        vmem((27, chans, chans), F32),
-        vmem((HALF, chans, chans), BF16),
-        vmem((HALF, chans, chans), BF16),
+        vmem((3, 9, chans, chans), F32),
+        vmem((CHUNKS, PER, chans, chans), BF16),
+        vmem((CHUNKS, PER, chans, chans), BF16),
         vmem((CHUNKS, n_rows, PER, own_o, chans), BF16),
         vmem((CHUNKS, n_rows, PER, own_o, chans), BF16),
         vmem((CHUNKS, nz, PER, own_o, chans), BF16),
@@ -478,19 +503,19 @@
         vmem((n_tm, 2, chans), F32),
         vmem((n_rows, 2, chans), F32),
         vmem((n_tm, 2, chans), F32),
-        dma((3,)), dma((5,)),
+        dma((5,)), dma((5,)),
         dma((5,)), dma((5,)), dma((5,)), dma((5,)),
         dma((n_rows,)), dma((n_rows,)), dma((n_tm,)), dma((n_tm,)),
         dma((n_rows,)), dma((n_rows,)), dma((n_tm,)), dma((n_tm,)),
-        dma((2,)), dma((2,)),
+        dma((CHUNKS,)), dma((CHUNKS,)),
         dma((CHUNKS, n_rows)), dma((CHUNKS, n_rows)),
         dma((CHUNKS, nz)), dma((CHUNKS, nz)),
         dma((CHUNKS,)), dma((CHUNKS,)),
     ]
     anywhere = pl.BlockSpec(memory_space=pl.ANY)
-    inside = pl.BlockSpec(memory_space=pltpu.VMEM)
+    stays = pl.BlockSpec(memory_space=pltpu.HBM)
     out = jax.ShapeDtypeStruct
-    of, ig, wg, gg, bg = pl.pallas_call(
+    made = pl.pallas_call(
         functools.partial(kernel, sizes),
         out_shape=(
             out(frames_in.shape, BF16),
@@ -499,7 +524,7 @@
             out((1, chans), F32),
             out((1, chans), F32),
         ),
-        in_specs=[anywhere, inside, inside, anywhere, anywhere],
+        in_specs=[stays] * 5,
         out_specs=(anywhere,) * 5,
         scratch_shapes=scratch,
         compiler_params=pltpu.CompilerParams(
@@ -507,12 +532,26 @@
         ),
         name="block",
     )(
-        frames_in,
-        norm_gain.reshape(1, chans),
-        norm_bias.reshape(1, chans),
-        conv_weight.reshape(27, chans, chans),
-        cotangent,
+        *(
+            pltpu.with_memory_space_constraint(a, pltpu.HBM)
+            for a in (
+                frames_in,
+                norm_gain.reshape(1, chans),
+                norm_bias.reshape(1, chans),
+                conv_weight.reshape(27, chans, chans),
+                cotangent,
+            )
+        )
     )
+    of, ig, wg, gg, bg = pl.pallas_call(
+        put_out,
+        out_shape=[out(a.shape, a.dtype) for a in made],
+        in_specs=[anywhere] * 5,
+        out_specs=[stays] * 5,
+        scratch_shapes=[dma((5,))],
+        compiler_params=pltpu.CompilerParams(vmem_limit_bytes=1 << 20),
+        name="put_out",
+    )(*made)
     return of, ig, wg, gg.reshape(chans), bg.reshape(chans)
 
 

time: 53.3 us -> 43.8 us (0.82)
  local copies, waits for them, and re-layouts: 6.76 us -> 0 us
  Pallas kernels: 45.7 us -> 43.1 us
    unnamed x15 -> x0, local copies, waits for them, and re-layouts: 6.76 us -> none
    pallas_call x1, Pallas kernels: 45.7 us -> 42.2 us  [per_device(): pl.pallas_call(functools.partial(kernel, sizes), out_shape=(out(frames_in...]
    pallas_call x0 -> x1, Pallas kernels: none -> 0.86 us  [per_device(): pl.pallas_call(put_out, out_shape=[out(a.shape, a.dtype) for a in made],...]
where the time goes in v2:
time: 43.8 us; the launch traced here: 43.7 us
  Pallas kernels  43.1 us (98%)
  between operations  0.64 us (1%)
    pallas_call x1, Pallas kernels, per_device(): pl.pallas_call(functools.partial(kernel, sizes), out_shape=(out(frames_in...  42.2 us

profile of v2, /device:TPU:1, one launch (start us, length us, event | category | flops | bytes accessed | tf_op | source)
XLA Modules:
  0.0 43.7 jit_solution(15392286226580007642)
XLA Ops:
  0.6 42.2 %block.1 = (bf16[2,4,120,128]{3,2,1,0:T(8,128)(2,1)S(1)}, bf16[2,4,120,128]{3,2,1,0:T(8,128)(2,1)S(1)}, f32[8,3456]{1,0:T(8,128)S(1)}, f32[1,128]{1,0:T(1,128)S(1)}, f32[1,128]{1,0:T(1,128)S(1)}) custom-call(bf16[2,4,120,128]{3,2,1,0:T(8,128)(2,1)} %x_hbm.1, f32[1,128]{1,0:T(1,128)} %bitcast.6, f32[1,128]{1,0:T(1,128)} %bitcast.7, ...), custom_call_target="tpu_custom_call" | custom-call | tf_op jit(solution)/shard_map/block/pallas_call | solution.py:518
  42.8 0.9 %put_out.1 = (bf16[2,4,120,128]{3,2,1,0:T(8,128)(2,1)}, bf16[2,4,120,128]{3,2,1,0:T(8,128)(2,1)}, f32[8,3456]{1,0:T(8,128)}, f32[1,128]{1,0:T(1,128)}, f32[1,128]{1,0:T(1,128)}) custom-call(bf16[2,4,120,128]{3,2,1,0:T(8,128)(2,1)S(1)} %get-tuple-element.15.refs_0_, bf16[2,4,120,128]{3,2,1,0:T(8,128)(2,1)S(1)} %get-tuple-element.16.refs_1_, ...), custom_call_target="tpu_custom_call" | custom-call | tf_op jit(solution)/shard_map/put_out/pallas_call | solution.py:546

commit v3 on v2

--- a/solution.py
+++ b/solution.py
@@ -17,6 +17,7 @@
 WP = 128
 CHUNKS = 3
 PER = 5
+PIECES = ((0, 0, 5), (1, 0, 5), (2, 0, 3), (2, 3, 2))
 F32 = jnp.float32
 BF16 = jnp.bfloat16
 
@@ -36,10 +37,10 @@
 
 def kernel(
     sizes, x_hbm, gn_hbm, sh_hbm, w_hbm, cot_hbm,
-    of_hbm, ig_hbm, wg_hbm, gain_hbm, bias_hbm,
+    ofv, igv, wgv, gv, bv,
     gain_ref, bias_ref, xr, cr, wv, a0, a3, c3, ct, ga, wgf, dsend, drecv, bsend, brecv, crecv, fin,
-    ofv, igv, wgv, gv, bv, st1, st2, gs1, gs2,
-    load_sem, out_sem, xs, xq, cs, cq, s1s, s1r, s2s, s2r, g1s, g1r, g2s, g2r,
+    st1, st2, gs1, gs2,
+    load_sem, xs, xq, cs, cq, s1s, s1r, s2s, s2r, g1s, g1r, g2s, g2r,
     ds, dr, bs, br, zs, zr, fs, fr,
 ):
     nz, nc, ny, nx = sizes
@@ -57,6 +58,8 @@
         t, r = lax.rem(t + n_tm, n_tm), lax.rem(r + n_rows, n_rows)
         return {"z": t // nc, "c": lax.rem(t, nc), "y": r // nx, "x": lax.rem(r, nx)}
 
+    other = {"z": z, "c": 1 - c, "y": y, "x": x}
+
     def xy_peers():
         for k in range(1, n_rows):
             dy, dx = k // nx, k % nx
@@ -114,23 +117,19 @@
 
     def spread_xy(slots, send_sem, recv_sem):
         return [
-            remote(slots.at[row], slots.at[row], send_sem.at[k], recv_sem.at[row], device)
-            for k, _, device in xy_peers()
+            remote(slots.at[row], slots.at[row], send_sem, recv_sem, device)
+            for _, _, device in xy_peers()
         ]
 
     def spread_zc(slots, send_sem, recv_sem):
         return [
-            remote(slots.at[tm], slots.at[tm], send_sem.at[k], recv_sem.at[tm], device)
-            for k, _, device in zc_peers()
+            remote(slots.at[tm], slots.at[tm], send_sem, recv_sem, device)
+            for _, _, device in zc_peers()
         ]
 
-    def arrived_xy(slots, send_sem, recv_sem):
-        for k, peer, device in xy_peers():
-            remote(slots.at[peer], slots.at[peer], send_sem.at[k], recv_sem.at[peer], device).wait_recv()
-
-    def arrived_zc(slots, send_sem, recv_sem):
-        for k, peer, device in zc_peers():
-            remote(slots.at[peer], slots.at[peer], send_sem.at[k], recv_sem.at[peer], device).wait_recv()
+    def all_but_one(slots, send_sem, recv_sem):
+        rest = slots.at[0 : slots.shape[0] - 1]
+        return remote(rest, rest, send_sem, recv_sem, other)
 
     def summed(slots):
         total = slots[0]
@@ -138,8 +137,7 @@
             total = total + slots[k]
         return total
 
-    sent = spread_xy(st1, s1s, s1r)
-    for copy in sent:
+    for copy in spread_xy(st1, s1s.at[0], s1r.at[0]):
         copy.start()
 
     def margins(buf, first, there, way, send_sem, recv_sem):
@@ -195,10 +193,9 @@
     load_gn.wait()
     load_sh.wait()
 
-    arrived_xy(st1, s1s, s1r)
+    all_but_one(st1, s1s.at[0], s1r.at[0]).wait_recv()
     st2[tm] = summed(st1)
-    sent2 = spread_zc(st2, s2s, s2r)
-    for copy in sent2:
+    for copy in spread_zc(st2, s2s.at[0], s2r.at[0]):
         copy.start()
 
     row_low, row_high = row > 0, row < n_rows - 1
@@ -249,7 +246,7 @@
     ga[0:half] += both[:, :chans]
     ga[half:] += back(frame(c3s, 3), back_taps(2)) + both[:, chans:]
 
-    arrived_zc(st2, s2s, s2r)
+    all_but_one(st2, s2s.at[0], s2r.at[0]).wait_recv()
     stats = summed(st2)
     wide = lambda v: jnp.broadcast_to(v, (8, chans))
     mean = group_total(wide(stats[0:1]), chans // G) / cells
@@ -280,9 +277,8 @@
         return carry
 
     def act_frames(low, high):
-        lax.fori_loop(low * (band + 2), high * (band + 2), act_row, 0)
-
-    other = {"z": z, "c": 1 - c, "y": y, "x": x}
+        lax.fori_loop(low * (band + 2), high * (band + 2), act_row, 0, unroll=True)
+
     given, kept = 4 * (1 - c), 4 * c
     halves = [
         remote(dsend.at[a], drecv.at[a], ds.at[a], dr.at[a], other) for a in range(CHUNKS)
@@ -299,26 +295,20 @@
             dsend[a, j] = wgf[a, given + j].astype(BF16)
         halves[a].start()
 
-    to_rows = []
-
-    def send_rows(a):
-        halves[a].wait_recv()
-        for j in range(PER):
+    def send_rows(p):
+        a, low, count = PIECES[p]
+        for j in range(low, low + count):
             value = wgf[a, kept + j] + drecv[a, j].astype(F32)
             bsend[a, :, j] = value.reshape(n_rows, own_o, chans).astype(BF16)
-        brecv[a, row] = bsend[a, row]
+        blocks = slice(low, low + count)
+        brecv[a, row, blocks] = bsend[a, row, blocks]
         for k, peer, device in xy_peers():
-            copy = remote(
-                bsend.at[a, peer], brecv.at[a, row], bs.at[a, k], br.at[a, row], device
-            )
-            copy.start()
-            to_rows.append(copy)
+            there = brecv.at[a, row, blocks]
+            remote(bsend.at[a, peer, blocks], there, bs.at[p], br.at[p], device).start()
 
     act_frames(0, 2)
     weight_blocks(0)
     act_frames(2, 3)
-    weight_blocks(1)
-
     def pre_row(k):
         v = xr[frames + k // band, 1 + lax.rem(k, band)].astype(F32)
         return (v - mean) * inverse
@@ -336,18 +326,23 @@
             biases + grad.reshape(width // 8, 8, chans).sum(axis=0),
         )
 
-    gains, biases = lax.fori_loop(0, frames * band, grad_row, (zero8, zero8))
+    gains, biases = lax.fori_loop(0, frames * band, grad_row, (zero8, zero8), unroll=True)
     gs1[row, 0:1] = gains.sum(axis=0, keepdims=True)
     gs1[row, 1:2] = biases.sum(axis=0, keepdims=True)
-    sent3 = spread_xy(gs1, g1s, g1r)
-    for copy in sent3:
-        copy.start()
-
+    for copy in spread_xy(gs1, g1s.at[0], g1r.at[0]):
+        copy.start()
+
+    weight_blocks(1)
+
+    halves[0].wait_recv()
     send_rows(0)
     act_frames(3, 4)
     weight_blocks(2)
+    halves[1].wait_recv()
     send_rows(1)
+    halves[2].wait_recv()
     send_rows(2)
+    send_rows(3)
 
     def shift_row(k, carry):
         t, h = k // (band + 2), lax.rem(k, band + 2)
@@ -374,40 +369,37 @@
     two = front(frame(sides, 2), jnp.concatenate([front_taps(2), front_taps(1)], axis=1))
     put_frame(0, front(frame(sides, 0), front_taps(0)) + one[:, :chans] + two[:, :chans])
     put_frame(1, front(frame(sides, 3), front_taps(2)) + one[:, chans:] + two[:, chans:])
-    put_of = pltpu.make_async_copy(ofv, of_hbm, out_sem.at[0])
-    put_of.start()
-
-    arrived_xy(gs1, g1s, g1r)
-    gs2[tm] = summed(gs1)
-    sent4 = spread_zc(gs2, g2s, g2r)
-    for copy in sent4:
-        copy.start()
-
-    to_z = []
-    for ch in range(CHUNKS):
-        for k, peer, device in xy_peers():
-            remote(
-                bsend.at[ch, peer], brecv.at[ch, peer], bs.at[ch, k], br.at[ch, peer], device
-            ).wait_recv()
-        value = brecv[ch, 0].astype(F32)
+
+    def piece(buf, p, send_sem, recv_sem):
+        a, low, count = PIECES[p]
+        return all_but_one(buf.at[a, :, low : low + count], send_sem.at[p], recv_sem.at[p])
+
+    def send_z(p):
+        piece(brecv, p, bs, br).wait_recv()
+        a, low, count = PIECES[p]
+        blocks = slice(low, low + count)
+        value = brecv[a, 0, blocks].astype(F32)
         for k in range(1, n_rows):
-            value = value + brecv[ch, k].astype(F32)
-        crecv[ch, z] = value.astype(BF16)
+            value = value + brecv[a, k, blocks].astype(F32)
+        crecv[a, z, blocks] = value.astype(BF16)
+        mine = crecv.at[a, z, blocks]
         for k in range(1, nz):
             device = {"z": lax.rem(z + k, nz), "c": c, "y": y, "x": x}
-            copy = remote(crecv.at[ch, z], crecv.at[ch, z], zs.at[ch, k], zr.at[ch, z], device)
-            copy.start()
-            to_z.append(copy)
-
-    arrived_zc(gs2, g2s, g2r)
+            remote(mine, mine, zs.at[p], zr.at[p], device).start()
+
+    all_but_one(gs1, g1s.at[0], g1r.at[0]).wait_recv()
+    gs2[tm] = summed(gs1)
+    for copy in spread_zc(gs2, g2s.at[0], g2r.at[0]):
+        copy.start()
+
+    for p in range(len(PIECES)):
+        send_z(p)
+
+    all_but_one(gs2, g2s.at[0], g2r.at[0]).wait_recv()
     sums = summed(gs2)
     gain_grad, bias_grad = wide(sums[0:1]), wide(sums[1:2])
     gv[...] = sums[0:1]
     bv[...] = sums[1:2]
-    put_g = pltpu.make_async_copy(gv, gain_hbm, out_sem.at[3])
-    put_b = pltpu.make_async_copy(bv, bias_hbm, out_sem.at[4])
-    put_g.start()
-    put_b.start()
     mean_dn = (group_total(gain * bias_grad, chans // G) / cells)[0:1]
     mean_dnn = (group_total(gain * gain_grad, chans // G) / cells)[0:1]
 
@@ -420,44 +412,45 @@
         return carry
 
     lax.fori_loop(0, frames * band, input_row, 0)
-    put_ig = pltpu.make_async_copy(igv, ig_hbm, out_sem.at[1])
-    put_ig.start()
 
     to_core = []
-    for ch in range(CHUNKS):
+    for p, (a, low, count) in enumerate(PIECES):
+        piece(crecv, p, zs, zr).wait_recv()
+        blocks = slice(low, low + count)
+        value = crecv[a, 0, blocks].astype(F32)
         for k in range(1, nz):
-            peer = lax.rem(z + k, nz)
-            device = {"z": peer, "c": c, "y": y, "x": x}
-            remote(
-                crecv.at[ch, peer], crecv.at[ch, peer], zs.at[ch, k], zr.at[ch, peer], device
-            ).wait_recv()
-        value = crecv[ch, 0].astype(F32)
-        for k in range(1, nz):
-            value = value + crecv[ch, k].astype(F32)
-        fin[c, ch] = value
-        copy = remote(fin.at[c, ch], fin.at[c, ch], fs.at[ch], fr.at[ch], other)
+            value = value + crecv[a, k, blocks].astype(F32)
+        fin[c, a, blocks] = value
+        mine = fin.at[c, a, blocks]
+        copy = remote(mine, mine, fs.at[p], fr.at[p], other)
         copy.start()
         to_core.append(copy)
-    for ch in range(CHUNKS):
-        remote(fin.at[1 - c, ch], fin.at[1 - c, ch], fs.at[ch], fr.at[ch], other).wait_recv()
     scale = 1.0 / math.sqrt(all_pixels)
-    for j in range(27):
-        a, m = j // 9, j % 9
-        value = fin[0, a, m] if m < PER else fin[1, a, m - 4]
-        wgv[:, j * chans : (j + 1) * chans] = value * scale
-    put_wg = pltpu.make_async_copy(wgv, wg_hbm, out_sem.at[2])
-    put_wg.start()
-
-    for copy in (*sent, *sent2, *sent3, *sent4, *halves, *to_rows, *to_z, *to_core):
+    for p, (a, low, count) in enumerate(PIECES):
+        theirs = fin.at[1 - c, a, low : low + count]
+        remote(theirs, theirs, fs.at[p], fr.at[p], other).wait_recv()
+        for core in range(2):
+            for j in range(low, low + count):
+                if core == 0 or j > 0:
+                    at_m = (9 * a + 4 * core + j) * chans
+                    wgv[:, at_m : at_m + chans] = fin[core, a, j] * scale
+
+    for copy in (
+        all_but_one(st1, s1s.at[0], s1r.at[0]),
+        all_but_one(st2, s2s.at[0], s2r.at[0]),
+        all_but_one(gs1, g1s.at[0], g1r.at[0]),
+        all_but_one(gs2, g2s.at[0], g2r.at[0]),
+        *halves,
+        *(piece(bsend, p, bs, br) for p in range(len(PIECES))),
+        *(piece(crecv, p, zs, zr) for p in range(len(PIECES))),
+        *to_core,
+    ):
         copy.wait_send()
     for copy, sends, _ in (*cot_margins, *x_margins):
 
         @pl.when(sends)
         def _():
             copy.wait_send()
-
-    for copy in (put_of, put_ig, put_g, put_b, put_wg):
-        copy.wait()
 
 
 def put_out(*refs):
@@ -494,23 +487,17 @@
         vmem((CHUNKS, n_rows, PER, own_o, chans), BF16),
         vmem((CHUNKS, nz, PER, own_o, chans), BF16),
         vmem((2, CHUNKS, PER, own_o, chans), F32),
-        vmem((frames, band, width, chans), BF16),
-        vmem((frames, band, width, chans), BF16),
-        vmem((own_o, 27 * chans), F32),
-        vmem((1, chans), F32),
-        vmem((1, chans), F32),
         vmem((n_rows, 2, chans), F32),
         vmem((n_tm, 2, chans), F32),
         vmem((n_rows, 2, chans), F32),
         vmem((n_tm, 2, chans), F32),
-        dma((5,)), dma((5,)),
+        dma((5,)),
         dma((5,)), dma((5,)), dma((5,)), dma((5,)),
-        dma((n_rows,)), dma((n_rows,)), dma((n_tm,)), dma((n_tm,)),
-        dma((n_rows,)), dma((n_rows,)), dma((n_tm,)), dma((n_tm,)),
+        dma((1,)), dma((1,)), dma((1,)), dma((1,)), dma((1,)), dma((1,)), dma((1,)), dma((1,)),
         dma((CHUNKS,)), dma((CHUNKS,)),
-        dma((CHUNKS, n_rows)), dma((CHUNKS, n_rows)),
-        dma((CHUNKS, nz)), dma((CHUNKS, nz)),
-        dma((CHUNKS,)), dma((CHUNKS,)),
+        dma((len(PIECES),)), dma((len(PIECES),)),
+        dma((len(PIECES),)), dma((len(PIECES),)),
+        dma((len(PIECES),)), dma((len(PIECES),)),
     ]
     anywhere = pl.BlockSpec(memory_space=pl.ANY)
     stays = pl.BlockSpec(memory_space=pltpu.HBM)
@@ -525,7 +512,7 @@
             out((1, chans), F32),
         ),
         in_specs=[stays] * 5,
-        out_specs=(anywhere,) * 5,
+        out_specs=[pl.BlockSpec(memory_space=pltpu.VMEM)] * 5,
         scratch_shapes=scratch,
         compiler_params=pltpu.CompilerParams(
             collective_id=0, has_side_effects=True, vmem_limit_bytes=48 << 20

time: 43.8 us -> 40.5 us (0.925)
  Pallas kernels: 43.1 us -> 39.8 us
    pallas_call x1, Pallas kernels: 42.2 us -> 38.9 us  [per_device(): pl.pallas_call(functools.partial(kernel, sizes), out_shape=(out(frames_in...]
where the time goes in v3:
time: 40.5 us; the launch traced here: 40.4 us
  Pallas kernels  39.8 us (98%)
  between operations  0.64 us (2%)
    pallas_call x1, Pallas kernels, per_device(): pl.pallas_call(functools.partial(kernel, sizes), out_shape=(out(frames_in...  38.9 us
    pallas_call x1, Pallas kernels, per_device(): pl.pallas_call(put_out, out_shape=[out(a.shape, a.dtype) for a in made],...  0.86 us

profile of v3, /device:TPU:1, one launch (start us, length us, event | category | flops | bytes accessed | tf_op | source)
XLA Modules:
  0.0 40.4 jit_solution(7966842049944203599)
XLA Ops:
  0.6 38.9 %block.1 = (bf16[2,4,120,128]{3,2,1,0:T(8,128)(2,1)S(1)}, bf16[2,4,120,128]{3,2,1,0:T(8,128)(2,1)S(1)}, f32[8,3456]{1,0:T(8,128)S(1)}, f32[1,128]{1,0:T(1,128)S(1)}, f32[1,128]{1,0:T(1,128)S(1)}) custom-call(bf16[2,4,120,128]{3,2,1,0:T(8,128)(2,1)} %x_hbm.1, f32[1,128]{1,0:T(1,128)} %bitcast.6, f32[1,128]{1,0:T(1,128)} %bitcast.7, ...), custom_call_target="tpu_custom_call" | custom-call | tf_op jit(solution)/shard_map/block/pallas_call | solution.py:505
  39.5 0.9 %put_out.1 = (bf16[2,4,120,128]{3,2,1,0:T(8,128)(2,1)}, bf16[2,4,120,128]{3,2,1,0:T(8,128)(2,1)}, f32[8,3456]{1,0:T(8,128)}, f32[1,128]{1,0:T(1,128)}, f32[1,128]{1,0:T(1,128)}) custom-call(bf16[2,4,120,128]{3,2,1,0:T(8,128)(2,1)S(1)} %get-tuple-element.15.refs_0_, bf16[2,4,120,128]{3,2,1,0:T(8,128)(2,1)S(1)} %get-tuple-element.16.refs_1_, ...), custom_call_target="tpu_custom_call" | custom-call | tf_op jit(solution)/shard_map/put_out/pallas_call | solution.py:533

commit v4 on v3

v4 whole, which is shorter than its diff:
```python
import functools
import math

import jax
import jax.numpy as jnp
from jax import lax
from jax.experimental import pallas as pl
from jax.experimental.pallas import tpu as pltpu
from jax.sharding import Mesh
from jax.sharding import PartitionSpec as P

G = 32
EPSILON = 1e-06
TM = ("z", "c")
ROWS = ("y", "x")
MESH = pl.DeviceIdType.MESH
WP = 128
F32 = jnp.float32
BF16 = jnp.bfloat16
PAIRS = tuple((a, b) for a in (2, 1, 0) for b in range(3))
PIECES = ((0, 1), (1, 3), (3, 5), (5, 7), (7, 9))
N_PIECES = len(PIECES)


def group_total(per_channel, size):
    lanes = lax.broadcasted_iota(jnp.int32, per_channel.shape, 1)
    within = lanes % size
    channels = per_channel.shape[1]
    total = per_channel
    for step in range(1, size):
        ahead = pltpu.roll(per_channel, channels - step, 1)
        behind = pltpu.roll(per_channel, step, 1)
        total = total + jnp.where(within + step < size, ahead, 0.0)
        total = total + jnp.where(within >= step, behind, 0.0)
    return total


def kernel(
    sizes, x_hbm, gn_hbm, sh_hbm, w_hbm, cot_hbm,
    ofv, igv, wgv, gv, bv,
    gain_ref, bias_ref, xr, cr, cpart, wv, a0, a3, c3, c3e, ct, ga, cv, bsend, brecv, crecv, fin,
    st1, st2, gs1, gs2,
    load_sem, xs, xq, cs, cq, ps, pq, st_s, st_r, bs, br, zs, zr, fs, fr,
):
    nz, nc, ny, nx = sizes
    n_tm, n_rows = nz * nc, ny * nx
    frames, band, width, chans = x_hbm.shape
    high_rows = band + 2
    own_o = chans // n_rows
    dests = n_rows // nc
    half_o = chans // nc
    all_pixels = frames * n_tm * band * n_rows * width
    cells = all_pixels * (chans // G)
    z, c = lax.axis_index("z"), lax.axis_index("c")
    y, x = lax.axis_index("y"), lax.axis_index("x")
    tm, row = z * nc + c, y * nx + x
    own = frames + frames * c
    other = {"z": z, "c": 1 - c, "y": y, "x": x}
    lead, follow = c == 0, c == 1
    has_before = z > 0

    def at(t, r):
        t, r = lax.rem(t + n_tm, n_tm), lax.rem(r + n_rows, n_rows)
        return {"z": t // nc, "c": lax.rem(t, nc), "y": r // nx, "x": lax.rem(r, nx)}

    def farthest_first(steps):
        return sorted(steps, key=lambda pairs: -sum(min(d, n - d) for d, n in pairs))

    def xy_peers():
        for (dy, _), (dx, _) in farthest_first(
            [((k // nx, ny), (k % nx, nx)) for k in range(1, n_rows)]
        ):
            ty, tx = lax.rem(y + dy, ny), lax.rem(x + dx, nx)
            yield {"z": z, "c": c, "y": ty, "x": tx}

    def zc_peers():
        for (dz, _), (dc, _) in farthest_first(
            [((k // nc, nz), (k % nc, nc)) for k in range(1, n_tm)]
        ):
            tz, tc = lax.rem(z + dz, nz), lax.rem(c + dc, nc)
            yield {"z": tz, "c": tc, "y": y, "x": x}

    def z_peers():
        for ((dz, _),) in farthest_first([((k, nz),) for k in range(1, nz)]):
            yield {"z": lax.rem(z + dz, nz), "c": c, "y": y, "x": x}

    def remote(src, dst, send_sem, recv_sem, device):
        return pltpu.make_async_remote_copy(
            src_ref=src, dst_ref=dst, send_sem=send_sem, recv_sem=recv_sem,
            device_id=device, device_id_type=MESH,
        )

    def several(slots, count, send_sem, recv_sem):
        some = slots.at[0:count]
        return remote(some, some, send_sem, recv_sem, other)

    load_x = pltpu.make_async_copy(
        x_hbm, xr.at[pl.ds(own, frames), 1 : band + 1], load_sem.at[0]
    )
    load_c = pltpu.make_async_copy(cot_hbm, cr.at[0:frames, 1 : band + 1], load_sem.at[1])
    load_w = pltpu.make_async_copy(w_hbm, wv, load_sem.at[2])
    load_gn = pltpu.make_async_copy(gn_hbm, gain_ref, load_sem.at[3])
    load_sh = pltpu.make_async_copy(sh_hbm, bias_ref, load_sem.at[4])
    for copy in (load_x, load_c, load_w, load_gn, load_sh):
        copy.start()

    barrier = pltpu.get_barrier_semaphore()
    partners = 0
    corners = [at(tm + dt, row + dw) for dt in (-1, 1) for dw in (-1, 1)]
    for device in (*zc_peers(), *xy_peers(), *corners):
        pl.semaphore_signal(barrier, inc=1, device_id=device, device_id_type=MESH)
        partners += 1

    load_x.wait()

    def folded(v):
        return v.reshape(width // 8, 8, chans).sum(axis=0)

    def stat_row(k, carry):
        total, square = carry
        v = xr[own + k // band, 1 + lax.rem(k, band)].astype(F32)
        return total + folded(v), square + folded(v * v)

    zero8 = jnp.zeros((8, chans), F32)
    total, square = lax.fori_loop(0, frames * band, stat_row, (zero8, zero8))
    st1[row, 0:1] = total.sum(axis=0, keepdims=True)
    st1[row, 1:2] = square.sum(axis=0, keepdims=True)

    pl.semaphore_wait(barrier, partners)

    def summed(slots):
        total = slots[0]
        for k in range(1, slots.shape[0]):
            total = total + slots[k]
        return total

    def spread(slots, mine, peers, k):
        for device in peers:
            remote(slots.at[mine], slots.at[mine], st_s.at[k], st_r.at[k], device).start()

    def gathered(slots, k):
        return several(slots, slots.shape[0] - 1, st_s.at[k], st_r.at[k])

    spread(st1, row, xy_peers(), 0)

    def margins(buf, first, there, way, sends_on, gets_on, send_sem, recv_sem):
        mine = buf.at[pl.ds(first, frames)]
        moved = buf.at[pl.ds(there, frames)]
        up_t = (tm + way >= 0) & (tm + way < n_tm) & sends_on
        from_t = (tm - way >= 0) & (tm - way < n_tm) & gets_on
        up_r, down_r = row < n_rows - 1, row > 0
        low, high, body = mine.at[:, 1], mine.at[:, band], slice(1, band + 1)
        plan = [
            (high, mine.at[:, 0], at(tm, row + 1), up_r, down_r),
            (low, mine.at[:, band + 1], at(tm, row - 1), down_r, up_r),
            (mine.at[:, body], moved.at[:, body], at(tm + way, row), up_t, from_t),
            (high, moved.at[:, 0], at(tm + way, row + 1), up_t & up_r, from_t & down_r),
            (low, moved.at[:, band + 1], at(tm + way, row - 1), up_t & down_r, from_t & up_r),
        ]
        return [
            (remote(src, dst, send_sem.at[k], recv_sem.at[k], device), sends, gets)
            for k, (src, dst, device, sends, gets) in enumerate(plan)
        ]

    load_c.wait()
    cot_margins = margins(cr, 0, frames, -1, True, True, cs, cq)
    x_margins = margins(xr, own, 0, 1, follow, lead, xs, xq)
    partner_cot = remote(cr.at[0:frames, 1 : band + 1], cpart, ps.at[0], pq.at[0], other)
    mine_x = xr.at[pl.ds(own, frames), 1 : band + 1]
    swapped_x = remote(mine_x, mine_x, ps.at[1], pq.at[1], other)

    def started(copy, sends):
        @pl.when(sends)
        def _():
            copy.start()

    def received(copy, gets):
        @pl.when(gets)
        def _():
            copy.wait_recv()

    def left(copy, sends):
        @pl.when(sends)
        def _():
            copy.wait_send()

    partner_cot.start()
    swapped_x.start()
    for copy, sends, _ in (*x_margins, *cot_margins):
        started(copy, sends)

    zeros_pad = jnp.zeros((WP - width, chans), F32)

    def padded_row(v):
        return jnp.concatenate([v, zeros_pad], axis=0)

    def three_ways(v, keep=True):
        v = padded_row(v.astype(F32))
        if keep is not True:
            v = jnp.where(keep, v, 0.0)
        return pltpu.roll(v, 1, 0), v, pltpu.roll(v, WP - 1, 0)

    def cot_row(t, h, keep=True):
        sides = three_ways(cr[t, h], keep)
        for shift in range(3):
            c3[shift, t, h] = sides[shift].astype(BF16)
        return sides

    def put_turned(chip_half, k, sides):
        for shift in range(3):
            turned = sides[2 - shift].T.astype(BF16)
            for core in range(nc):
                ct[chip_half, core, shift * half_o : (shift + 1) * half_o, k * WP : (k + 1) * WP] = (
                    turned[core * half_o : (core + 1) * half_o]
                )

    for k in range(frames * band):
        put_turned(c, k, cot_row(k // band, 1 + k % band))
    for h in (0, band + 1):
        c3[:, :, h] = jnp.zeros((3, 2 * frames, WP, chans), BF16)
    load_w.wait()
    load_gn.wait()
    load_sh.wait()
    partner_cot.wait_recv()
    for k in range(frames * band):
        put_turned(1 - c, k, three_ways(cpart[k // band, k % band]))

    gathered(st1, 0).wait_recv()
    st2[tm] = summed(st1)
    spread(st2, tm, zc_peers(), 1)

    row_low, row_high = row > 0, row < n_rows - 1
    before = xr.at[0:frames]
    passed_low = remote(before.at[:, 0], before.at[:, 0], ps.at[5], pq.at[5], other)
    passed_high = remote(before.at[:, band + 1], before.at[:, band + 1], ps.at[6], pq.at[6], other)
    body_before = before.at[:, 1 : band + 1]
    passed_body = remote(body_before, body_before, ps.at[4], pq.at[4], other)
    mine_all = xr.at[pl.ds(own, frames)]
    gave_low = remote(mine_all.at[:, 0], mine_all.at[:, 0], ps.at[2], pq.at[2], other)
    gave_high = remote(mine_all.at[:, band + 1], mine_all.at[:, band + 1], ps.at[3], pq.at[3], other)
    for copy, _, gets in x_margins[:2]:
        received(copy, gets)
    started(gave_low, row_low)
    started(gave_high, row_high)

    taps = [(b, s) for b in range(3) for s in range(3)]

    def frame(refs, t):
        rows = [refs[s][t, b : b + band].reshape(band * WP, chans) for b, s in taps]
        return jnp.concatenate(rows, axis=1)

    def back_taps(a):
        return jnp.concatenate([wv[9 * (2 - a) + 3 * (2 - b) + 2 - s] for b, s in taps], axis=1)

    def back(lhs, rhs):
        return lax.dot_general(lhs, rhs, (((1,), (1,)), ((), ())), preferred_element_type=F32)

    half = band * WP
    c3s = [c3.at[s] for s in range(3)]
    both = back(frame(c3s, 1), jnp.concatenate([back_taps(1), back_taps(0)], axis=0))
    ga[0:half] = back(frame(c3s, 0), back_taps(0)) + both[:, :chans]
    ga[half:] = both[:, chans:]

    received(cot_margins[2][0], cot_margins[2][2])
    has_next = tm < n_tm - 1
    for t in range(frames, 2 * frames):
        for h in range(1, band + 1):
            cot_row(t, h, has_next)
    both = back(frame(c3s, 2), jnp.concatenate([back_taps(2), back_taps(1)], axis=0))
    ga[0:half] += both[:, :chans]
    ga[half:] += back(frame(c3s, 3), back_taps(2)) + both[:, chans:]

    gathered(st2, 1).wait_recv()
    stats = summed(st2)
    wide = lambda v: jnp.broadcast_to(v, (8, chans))
    mean = group_total(wide(stats[0:1]), chans // G) / cells
    variance = group_total(wide(stats[1:2]), chans // G) / cells - mean * mean
    inverse = lax.rsqrt(variance + EPSILON)
    gain, shift_ = wide(gain_ref[...]), wide(bias_ref[...])
    mean, inverse, gain, shift_ = (v[0:1] for v in (mean, inverse, gain, shift_))

    swapped_x.wait_recv()
    received(gave_low, row_low)
    received(gave_high, row_high)

    def sigmoid(v):
        return 0.5 + 0.5 * jnp.tanh(0.5 * v)

    def act_frames(low, high, rows=range(band + 2)):
        for t in range(low, high):
            for h in rows:
                v = xr[t, h].astype(F32)
                pre = (v - mean) * inverse * gain + shift_
                act = pre * sigmoid(pre)
                keep = True
                if t < frames:
                    keep = has_before
                if h == 0:
                    keep = keep & row_low
                if h == band + 1:
                    keep = keep & row_high
                if keep is not True:
                    act = jnp.where(keep, act, 0.0)
                a0[t, h] = padded_row(act).astype(BF16)

    chip_frames = frames * nc
    turned = lambda: jnp.concatenate([ct[h, c] for h in range(nc)], axis=1)
    active = row // dests == c
    place = lax.rem(row, dests)

    def blocks_of(p):
        low, high = PIECES[p]
        return slice(3 * low, 3 * high)

    def weight_piece(p):
        low, high = PIECES[p]
        rhs = jnp.concatenate(
            [
                a0[a : a + chip_frames, b : b + band].reshape(chip_frames * half, chans)
                for a, b in PAIRS[low:high]
            ],
            axis=1,
        )
        part = jnp.dot(turned(), rhs, preferred_element_type=F32)
        for j in range(high - low):
            for s in range(3):
                block = part[s * half_o : (s + 1) * half_o, j * chans : (j + 1) * chans]
                bsend[:, 3 * (low + j) + s] = block.reshape(dests, own_o, chans).astype(BF16)

    def send_rows(p):
        blocks = blocks_of(p)

        @pl.when(active)
        def _():
            brecv[row, blocks] = bsend[place, blocks]

        for q in range(dests):
            to = dests * c + q
            device = {"z": z, "c": c, "y": to // nx, "x": lax.rem(to, nx)}
            copy = remote(
                bsend.at[q, blocks], brecv.at[row, blocks], bs.at[p], br.at[p], device
            )
            started(copy, to != row)

    act_frames(frames, frames + chip_frames, range(band))
    for copy, _, gets in x_margins[2:]:
        received(copy, gets)
    started(passed_body, lead & has_before)
    started(passed_low, lead & has_before & row_low)
    started(passed_high, lead & has_before & row_high)

    weight_piece(0)
    send_rows(0)
    act_frames(frames, frames + chip_frames, range(band, band + 2))
    weight_piece(1)
    send_rows(1)
    received(passed_body, follow & has_before)
    received(passed_low, follow & has_before & row_low)
    received(passed_high, follow & has_before & row_high)
    act_frames(1, 2)

    weight_piece(2)
    send_rows(2)
    act_frames(0, 1)
    for k in (0, 1, 3, 4):
        received(cot_margins[k][0], cot_margins[k][2])
    for t in range(2 * frames):
        for side, exists in ((0, row_low), (1, row_high)):
            keep = exists & has_next if t >= frames else exists
            sides = three_ways(cr[t, side * (band + 1)], keep)
            for shift in range(3):
                c3e[shift, t, side] = sides[shift].astype(BF16)
    for side, b in ((0, 0), (1, 2)):
        lhs = jnp.concatenate(
            [
                jnp.concatenate(
                    [c3e[s, t + a, side] for a in range(3) for s in range(3)], axis=1
                )
                for t in range(frames)
            ],
            axis=0,
        )
        rhs = jnp.concatenate(
            [wv[9 * (2 - a) + 3 * (2 - b) + 2 - s] for a in range(3) for s in range(3)], axis=1
        )
        edge = back(lhs, rhs)
        for t in range(frames):
            at_t = t * half + side * (band - 1) * WP
            ga[at_t : at_t + WP] += edge[t * WP : (t + 1) * WP]

    def pre_row(k):
        v = xr[own + k // band, 1 + k % band].astype(F32)
        return (v - mean) * inverse

    gains, biases = zero8, zero8
    for k in range(frames * band):
        normed = pre_row(k)
        pre = normed * gain + shift_
        sig = sigmoid(pre)
        at_k = slice(k * WP, k * WP + width)
        grad = ga[at_k] * sig * (1.0 + pre * (1.0 - sig))
        ga[at_k] = grad
        gains = gains + folded(grad * normed)
        biases = biases + folded(grad)
    gs1[tm, 0:1] = gains.sum(axis=0, keepdims=True)
    gs1[tm, 1:2] = biases.sum(axis=0, keepdims=True)
    spread(gs1, tm, zc_peers(), 2)

    weight_piece(3)
    send_rows(3)
    weight_piece(4)
    send_rows(4)

    def of_piece(buf, count, p, send_sem, recv_sem):
        blocks = blocks_of(p)
        return several(buf.at[:, blocks], count, send_sem.at[p], recv_sem.at[p])

    def send_z(p):
        blocks = blocks_of(p)

        @pl.when(active)
        def _():
            of_piece(brecv, n_rows - 1, p, bs, br).wait_recv()
            value = brecv[0, blocks].astype(F32)
            for k in range(1, n_rows):
                value = value + brecv[k, blocks].astype(F32)
            crecv[z, blocks] = value.astype(BF16)
            mine = crecv.at[z, blocks]
            for device in z_peers():
                remote(mine, mine, zs.at[p], zr.at[p], device).start()

    def shift_row(k, carry):
        t, h = k // high_rows, lax.rem(k, high_rows)
        v = a0[frames * c + t, h].astype(F32)
        a3[0, t, h] = pltpu.roll(v, 1, 0).astype(BF16)
        a3[1, t, h] = pltpu.roll(v, WP - 1, 0).astype(BF16)
        return carry

    lax.fori_loop(0, 2 * frames * high_rows, shift_row, 0)
    send_z(0)
    sides = (a3.at[0], a0.at[pl.ds(frames * c, 2 * frames)], a3.at[1])

    def front_taps(a):
        return jnp.concatenate([wv[9 * a + 3 * b + s] for b, s in taps], axis=0)

    def front(lhs, rhs):
        return jnp.dot(lhs, rhs, preferred_element_type=F32)

    one = front(frame(sides, 1), jnp.concatenate([front_taps(1), front_taps(0)], axis=1))
    cv[0:half] = front(frame(sides, 0), front_taps(0)) + one[:, :chans]
    cv[half:] = one[:, chans:]
    send_z(1)
    two = front(frame(sides, 2), jnp.concatenate([front_taps(2), front_taps(1)], axis=1))
    cv[0:half] += two[:, :chans]
    cv[half:] += front(frame(sides, 3), front_taps(2)) + two[:, chans:]
    for k in range(frames * band):
        v = xr[own + k // band, 1 + k % band].astype(F32)
        ofv[k // band, k % band] = (v + cv[k * WP : k * WP + width]).astype(BF16)
    send_z(2)
    gathered(gs1, 2).wait_recv()
    gs2[row] = summed(gs1)
    spread(gs2, row, xy_peers(), 3)

    send_z(3)

    send_z(4)

    gathered(gs2, 3).wait_recv()
    sums = summed(gs2)
    gain_grad, bias_grad = wide(sums[0:1]), wide(sums[1:2])
    gv[...] = sums[0:1]
    bv[...] = sums[1:2]
    mean_dn = (group_total(gain * bias_grad, chans // G) / cells)[0:1]
    mean_dnn = (group_total(gain * gain_grad, chans // G) / cells)[0:1]
    for k in range(frames * band):
        t, h = k // band, k % band
        normed = pre_row(k)
        grad = ga[k * WP : k * WP + width]
        cot = cr[t, 1 + h].astype(F32)
        igv[t, h] = (inverse * (grad * gain - mean_dn - normed * mean_dnn) + cot).astype(BF16)

    to_core = []
    for p in range(N_PIECES):
        blocks = blocks_of(p)
        mine = fin.at[blocks]
        copy = remote(mine, mine, fs.at[p], fr.at[p], other)
        to_core.append(copy)

        @pl.when(active)
        def _():
            of_piece(crecv, nz - 1, p, zs, zr).wait_recv()
            value = crecv[0, blocks].astype(F32)
            for k in range(1, nz):
                value = value + crecv[k, blocks].astype(F32)
            fin[blocks] = value
            copy.start()

    scale = 1.0 / math.sqrt(all_pixels)
    for p in range(N_PIECES):
        blocks = blocks_of(p)
        received(to_core[p], jnp.logical_not(active))
        for m in range(blocks.start, blocks.stop):
            a, b = PAIRS[m // 3]
            at_m = (9 * a + 3 * b + m % 3) * chans
            wgv[:, at_m : at_m + chans] = fin[m] * scale

    for slots, k in ((st1, 0), (st2, 1), (gs1, 2), (gs2, 3)):
        gathered(slots, k).wait_send()
    partner_cot.wait_send()
    swapped_x.wait_send()
    for copy, sends, _ in (*cot_margins, *x_margins):
        left(copy, sends)
    left(gave_low, row_low)
    left(gave_high, row_high)
    left(passed_body, lead & has_before)
    left(passed_low, lead & has_before & row_low)
    left(passed_high, lead & has_before & row_high)

    @pl.when(active)
    def _():
        for p in range(N_PIECES):
            of_piece(bsend, dests - 1, p, bs, br).wait_send()
            of_piece(crecv, nz - 1, p, zs, zr).wait_send()
            to_core[p].wait_send()

    @pl.when(jnp.logical_not(active))
    def _():
        for p in range(N_PIECES):
            of_piece(bsend, dests, p, bs, br).wait_send()


def put_out(*refs):
    sources, places, sem = refs[:5], refs[5:10], refs[10]
    copies = [pltpu.make_async_copy(s, d, sem.at[k]) for k, (s, d) in enumerate(zip(sources, places))]
    for copy in copies:
        copy.start()
    for copy in copies:
        copy.wait()


def per_device(sizes, frames_in, norm_gain, norm_bias, conv_weight, cotangent):
    nz, nc, ny, nx = sizes
    n_tm, n_rows = nz * nc, ny * nx
    frames, band, width, chans = frames_in.shape
    own_o, dests = chans // n_rows, n_rows // nc
    rows = (2 * frames, band + 2)
    chip = (frames + frames * nc, band + 2)
    vmem, dma = pltpu.VMEM, pltpu.SemaphoreType.DMA
    scratch = [
        vmem((1, chans), F32),
        vmem((1, chans), F32),
        vmem((*chip, width, chans), BF16),
        vmem((*rows, width, chans), BF16),
        vmem((frames, band, width, chans), BF16),
        vmem((27, chans, chans), BF16),
        vmem((*chip, WP, chans), BF16),
        vmem((2, *rows, WP, chans), BF16),
        vmem((3, *rows, WP, chans), BF16),
        vmem((3, 2 * frames, 2, WP, chans), BF16),
        vmem((nc, nc, 3 * chans // nc, frames * band * WP), BF16),
        vmem((frames * band * WP, chans), F32),
        vmem((frames * band * WP, chans), F32),
        vmem((dests, 27, own_o, chans), BF16),
        vmem((n_rows, 27, own_o, chans), BF16),
        vmem((nz, 27, own_o, chans), BF16),
        vmem((27, own_o, chans), F32),
        vmem((n_rows, 2, chans), F32),
        vmem((n_tm, 2, chans), F32),
        vmem((n_tm, 2, chans), F32),
        vmem((n_rows, 2, chans), F32),
        dma((5,)),
        dma((5,)), dma((5,)), dma((5,)), dma((5,)), dma((7,)), dma((7,)), dma((4,)), dma((4,)),
        dma((N_PIECES,)), dma((N_PIECES,)), dma((N_PIECES,)), dma((N_PIECES,)),
        dma((N_PIECES,)), dma((N_PIECES,)),
    ]
    anywhere = pl.BlockSpec(memory_space=pl.ANY)
    stays = pl.BlockSpec(memory_space=pltpu.HBM)
    inside = pl.BlockSpec(memory_space=pltpu.VMEM)
    out = jax.ShapeDtypeStruct
    operands = (
        frames_in,
        norm_gain.reshape(1, chans),
        norm_bias.reshape(1, chans),
        conv_weight.reshape(27, chans, chans),
        cotangent,
    )
    made = pl.pallas_call(
        functools.partial(kernel, sizes),
        out_shape=(
            out(frames_in.shape, BF16),
            out(frames_in.shape, BF16),
            out((own_o, 27 * chans), F32),
            out((1, chans), F32),
            out((1, chans), F32),
        ),
        in_specs=[stays] * 5,
        out_specs=[inside] * 5,
        scratch_shapes=scratch,
        compiler_params=pltpu.CompilerParams(
            collective_id=0, has_side_effects=True, vmem_limit_bytes=48 << 20
        ),
        name="block",
    )(*(pltpu.with_memory_space_constraint(a, pltpu.HBM) for a in operands))
    of, ig, wg, gg, bg = pl.pallas_call(
        put_out,
        out_shape=[out(a.shape, a.dtype) for a in made],
        in_specs=[anywhere] * 5,
        out_specs=[stays] * 5,
        scratch_shapes=[dma((5,))],
        compiler_params=pltpu.CompilerParams(vmem_limit_bytes=1 << 20),
        name="put_out",
    )(*made)
    return of, ig, wg, gg.reshape(chans), bg.reshape(chans)


def program(devices):
    torus = Mesh(devices, ("z", "c", "y", "x"))
    placed = (P(TM, ROWS, None, None), P(), P(), P(), P(TM, ROWS, None, None))
    return jax.shard_map(
        functools.partial(per_device, devices.shape),
        mesh=torus,
        in_specs=placed,
        out_specs=(P(TM, ROWS, None, None), P(TM, ROWS, None, None), P(ROWS, None), P(), P()),
        check_vma=False,
    )


def solution(mesh):
    return program(mesh.devices.reshape(8, 2, 4, 4))
```

time: 40.5 us -> 38.5 us (0.951)
  Pallas kernels: 39.8 us -> 37.8 us
    pallas_call x1, Pallas kernels: 38.9 us -> 37 us  [per_device(): pl.pallas_call(functools.partial(kernel, sizes), out_shape=(out(frames_in...]
where the time goes in v4:
time: 38.5 us
  Pallas kernels  37.8 us (98%)
  between operations  0.64 us (2%)
    pallas_call x1, Pallas kernels, per_device(): pl.pallas_call(functools.partial(kernel, sizes), out_shape=(out(frames_in...  37 us
    pallas_call x1, Pallas kernels, per_device(): pl.pallas_call(put_out, out_shape=[out(a.shape, a.dtype) for a in made],...  0.86 us

profile of v4, /device:TPU:1, one launch (start us, length us, event | category | flops | bytes accessed | tf_op | source)
XLA Modules:
  0.0 38.5 jit_solution(7885434978365801152)
XLA Ops:
  0.6 37.0 %block.1 = (bf16[2,4,120,128]{3,2,1,0:T(8,128)(2,1)S(1)}, bf16[2,4,120,128]{3,2,1,0:T(8,128)(2,1)S(1)}, f32[8,3456]{1,0:T(8,128)S(1)}, f32[1,128]{1,0:T(1,128)S(1)}, f32[1,128]{1,0:T(1,128)S(1)}) custom-call(bf16[2,4,120,128]{3,2,1,0:T(8,128)(2,1)} %x_hbm.1, f32[1,128]{1,0:T(1,128)} %bitcast.6, f32[1,128]{1,0:T(1,128)} %bitcast.7, ...), custom_call_target="tpu_custom_call" | custom-call | tf_op jit(solution)/shard_map/block/pallas_call | solution.py:587
  37.6 0.9 %put_out.1 = (bf16[2,4,120,128]{3,2,1,0:T(8,128)(2,1)}, bf16[2,4,120,128]{3,2,1,0:T(8,128)(2,1)}, f32[8,3456]{1,0:T(8,128)}, f32[1,128]{1,0:T(1,128)}, f32[1,128]{1,0:T(1,128)}) custom-call(bf16[2,4,120,128]{3,2,1,0:T(8,128)(2,1)S(1)} %get-tuple-element.15.refs_0_, bf16[2,4,120,128]{3,2,1,0:T(8,128)(2,1)S(1)} %get-tuple-element.16.refs_1_, ...), custom_call_target="tpu_custom_call" | custom-call | tf_op jit(solution)/shard_map/put_out/pallas_call | solution.py:604

commit v5 on v4

--- a/solution.py
+++ b/solution.py
@@ -18,7 +18,7 @@
 F32 = jnp.float32
 BF16 = jnp.bfloat16
 PAIRS = tuple((a, b) for a in (2, 1, 0) for b in range(3))
-PIECES = ((0, 1), (1, 3), (3, 5), (5, 7), (7, 9))
+PIECES = ((0, 1), (1, 3), (3, 5), (5, 7), (7, 8), (8, 9))
 N_PIECES = len(PIECES)
 
 
@@ -66,23 +66,14 @@
     def farthest_first(steps):
         return sorted(steps, key=lambda pairs: -sum(min(d, n - d) for d, n in pairs))
 
-    def xy_peers():
-        for (dy, _), (dx, _) in farthest_first(
-            [((k // nx, ny), (k % nx, nx)) for k in range(1, n_rows)]
-        ):
-            ty, tx = lax.rem(y + dy, ny), lax.rem(x + dx, nx)
-            yield {"z": z, "c": c, "y": ty, "x": tx}
-
-    def zc_peers():
-        for (dz, _), (dc, _) in farthest_first(
-            [((k // nc, nz), (k % nc, nc)) for k in range(1, n_tm)]
-        ):
-            tz, tc = lax.rem(z + dz, nz), lax.rem(c + dc, nc)
-            yield {"z": tz, "c": tc, "y": y, "x": x}
-
-    def z_peers():
+    def plane(core):
+        steps = [((k // nx, ny), (k % nx, nx)) for k in range(1, n_rows)]
+        for (dy, _), (dx, _) in farthest_first(steps):
+            yield {"z": z, "c": core, "y": lax.rem(y + dy, ny), "x": lax.rem(x + dx, nx)}
+
+    def column(core):
         for ((dz, _),) in farthest_first([((k, nz),) for k in range(1, nz)]):
-            yield {"z": lax.rem(z + dz, nz), "c": c, "y": y, "x": x}
+            yield {"z": lax.rem(z + dz, nz), "c": core, "y": y, "x": x}
 
     def remote(src, dst, send_sem, recv_sem, device):
         return pltpu.make_async_remote_copy(
@@ -93,6 +84,21 @@
     def several(slots, count, send_sem, recv_sem):
         some = slots.at[0:count]
         return remote(some, some, send_sem, recv_sem, other)
+
+    def started(copy, sends):
+        @pl.when(sends)
+        def _():
+            copy.start()
+
+    def received(copy, gets):
+        @pl.when(gets)
+        def _():
+            copy.wait_recv()
+
+    def left(copy, sends):
+        @pl.when(sends)
+        def _():
+            copy.wait_send()
 
     load_x = pltpu.make_async_copy(
         x_hbm, xr.at[pl.ds(own, frames), 1 : band + 1], load_sem.at[0]
@@ -105,11 +111,23 @@
         copy.start()
 
     barrier = pltpu.get_barrier_semaphore()
-    partners = 0
+    def enter(devices):
+        for device in devices:
+            pl.semaphore_signal(barrier, inc=1, device_id=device, device_id_type=MESH)
+
     corners = [at(tm + dt, row + dw) for dt in (-1, 1) for dw in (-1, 1)]
-    for device in (*zc_peers(), *xy_peers(), *corners):
-        pl.semaphore_signal(barrier, inc=1, device_id=device, device_id_type=MESH)
-        partners += 1
+    enter((*column(1), *plane(1), other, *corners))
+
+    @pl.when(follow)
+    def _():
+        enter((*column(0), *plane(0)))
+
+    @pl.when(lead)
+    def _():
+        enter((at(tm, row + 1), at(tm, row - 1)))
+
+    chips = n_rows - 1 + nz - 1
+    partners = jnp.where(follow, 2 * chips + 5, chips + 7)
 
     load_x.wait()
 
@@ -123,8 +141,8 @@
 
     zero8 = jnp.zeros((8, chans), F32)
     total, square = lax.fori_loop(0, frames * band, stat_row, (zero8, zero8))
-    st1[row, 0:1] = total.sum(axis=0, keepdims=True)
-    st1[row, 1:2] = square.sum(axis=0, keepdims=True)
+    st1[nc * row + c, 0:1] = total.sum(axis=0, keepdims=True)
+    st1[nc * row + c, 1:2] = square.sum(axis=0, keepdims=True)
 
     pl.semaphore_wait(barrier, partners)
 
@@ -134,28 +152,43 @@
             total = total + slots[k]
         return total
 
-    def spread(slots, mine, peers, k):
+    def collect(slots, mine, peers, k):
+        part = slots.at[mine]
         for device in peers:
-            remote(slots.at[mine], slots.at[mine], st_s.at[k], st_r.at[k], device).start()
-
-    def gathered(slots, k):
-        return several(slots, slots.shape[0] - 1, st_s.at[k], st_r.at[k])
-
-    spread(st1, row, xy_peers(), 0)
-
-    def margins(buf, first, there, way, sends_on, gets_on, send_sem, recv_sem):
+            remote(part, part, st_s.at[k], st_r.at[k], device).start()
+        started(remote(part, part, st_s.at[k], st_r.at[k], other), lead)
+
+    def spread(slots, mine, collected, peers, k):
+        @pl.when(follow)
+        def _():
+            several(collected, collected.shape[0] - 1, st_s.at[k - 1], st_r.at[k - 1]).wait_recv()
+            slots[mine] = summed(collected)
+            part = slots.at[mine]
+            for device in (*peers, other):
+                remote(part, part, st_s.at[k], st_r.at[k], device).start()
+
+    def finished(slots, k):
+        received(several(slots, slots.shape[0] - 1, st_s.at[k], st_r.at[k]), follow)
+        received(several(slots, slots.shape[0], st_s.at[k], st_r.at[k]), lead)
+
+    collect(st1, nc * row + c, plane(1), 0)
+
+    def margins(buf, first, there, way, body_from, corners_from, send_sem, recv_sem):
         mine = buf.at[pl.ds(first, frames)]
         moved = buf.at[pl.ds(there, frames)]
-        up_t = (tm + way >= 0) & (tm + way < n_tm) & sends_on
-        from_t = (tm - way >= 0) & (tm - way < n_tm) & gets_on
+        up_t = (tm + way >= 0) & (tm + way < n_tm)
+        from_t = (tm - way >= 0) & (tm - way < n_tm)
+        up_c, from_c = up_t & (c == corners_from), from_t & (c != corners_from)
+        if body_from is not None:
+            up_t, from_t = up_t & (c == body_from), from_t & (c != body_from)
         up_r, down_r = row < n_rows - 1, row > 0
         low, high, body = mine.at[:, 1], mine.at[:, band], slice(1, band + 1)
         plan = [
             (high, mine.at[:, 0], at(tm, row + 1), up_r, down_r),
             (low, mine.at[:, band + 1], at(tm, row - 1), down_r, up_r),
             (mine.at[:, body], moved.at[:, body], at(tm + way, row), up_t, from_t),
-            (high, moved.at[:, 0], at(tm + way, row + 1), up_t & up_r, from_t & down_r),
-            (low, moved.at[:, band + 1], at(tm + way, row - 1), up_t & down_r, from_t & up_r),
+            (high, moved.at[:, 0], at(tm + way, row + 1), up_c & up_r, from_c & down_r),
+            (low, moved.at[:, band + 1], at(tm + way, row - 1), up_c & down_r, from_c & up_r),
         ]
         return [
             (remote(src, dst, send_sem.at[k], recv_sem.at[k], device), sends, gets)
@@ -163,26 +196,11 @@
         ]
 
     load_c.wait()
-    cot_margins = margins(cr, 0, frames, -1, True, True, cs, cq)
-    x_margins = margins(xr, own, 0, 1, follow, lead, xs, xq)
+    cot_margins = margins(cr, 0, frames, -1, None, 0, cs, cq)
+    x_margins = margins(xr, own, 0, 1, 1, 1, xs, xq)
     partner_cot = remote(cr.at[0:frames, 1 : band + 1], cpart, ps.at[0], pq.at[0], other)
     mine_x = xr.at[pl.ds(own, frames), 1 : band + 1]
     swapped_x = remote(mine_x, mine_x, ps.at[1], pq.at[1], other)
-
-    def started(copy, sends):
-        @pl.when(sends)
-        def _():
-            copy.start()
-
-    def received(copy, gets):
-        @pl.when(gets)
-        def _():
-            copy.wait_recv()
-
-    def left(copy, sends):
-        @pl.when(sends)
-        def _():
-            copy.wait_send()
 
     partner_cot.start()
     swapped_x.start()
@@ -225,9 +243,7 @@
     for k in range(frames * band):
         put_turned(1 - c, k, three_ways(cpart[k // band, k % band]))
 
-    gathered(st1, 0).wait_recv()
-    st2[tm] = summed(st1)
-    spread(st2, tm, zc_peers(), 1)
+    spread(st2, z, st1, (*column(1), *column(0)), 1)
 
     row_low, row_high = row > 0, row < n_rows - 1
     before = xr.at[0:frames]
@@ -261,6 +277,16 @@
     ga[0:half] = back(frame(c3s, 0), back_taps(0)) + both[:, :chans]
     ga[half:] = both[:, chans:]
 
+    def cot_corner(h, k):
+        landing = cr.at[frames : 2 * frames, h]
+        return remote(cr.at[0:frames, h], landing, ps.at[k], pq.at[k], other)
+
+    cot_low, cot_high = cot_corner(0, 7), cot_corner(band + 1, 8)
+    for copy, _, gets in cot_margins[:2]:
+        received(copy, gets)
+    started(cot_low, follow & row_low)
+    started(cot_high, follow & row_high)
+
     received(cot_margins[2][0], cot_margins[2][2])
     has_next = tm < n_tm - 1
     for t in range(frames, 2 * frames):
@@ -270,7 +296,7 @@
     ga[0:half] += both[:, :chans]
     ga[half:] += back(frame(c3s, 3), back_taps(2)) + both[:, chans:]
 
-    gathered(st2, 1).wait_recv()
+    finished(st2, 1)
     stats = summed(st2)
     wide = lambda v: jnp.broadcast_to(v, (8, chans))
     mean = group_total(wide(stats[0:1]), chans // G) / cells
@@ -305,7 +331,7 @@
 
     chip_frames = frames * nc
     turned = lambda: jnp.concatenate([ct[h, c] for h in range(nc)], axis=1)
-    active = row // dests == c
+    in_first_half = row // dests == 0
     place = lax.rem(row, dests)
 
     def blocks_of(p):
@@ -327,20 +353,33 @@
                 block = part[s * half_o : (s + 1) * half_o, j * chans : (j + 1) * chans]
                 bsend[:, 3 * (low + j) + s] = block.reshape(dests, own_o, chans).astype(BF16)
 
+    ys = dests // nx
+    from_first = lax.rem(y - ys * c + ny, ny)
+
+    def band_dests():
+        near_first = (from_first == 0) | (from_first == ny - 1)
+        start = jnp.where(near_first, ys - 1, 0)
+        for ((dx, _),) in farthest_first([((k, nx),) for k in range(nx)]):
+            for j in range(ys):
+                yield ys * c + lax.rem(start + j, ys), lax.rem(x + dx, nx), dx != 0
+
     def send_rows(p):
         blocks = blocks_of(p)
 
-        @pl.when(active)
+        @pl.when(follow & jnp.logical_not(in_first_half))
         def _():
             brecv[row, blocks] = bsend[place, blocks]
 
-        for q in range(dests):
-            to = dests * c + q
-            device = {"z": z, "c": c, "y": to // nx, "x": lax.rem(to, nx)}
+        for ty, tx, is_other in band_dests():
+            q = (ty - ys * c) * nx + tx
+            device = {"z": z, "c": 1, "y": ty, "x": tx}
             copy = remote(
                 bsend.at[q, blocks], brecv.at[row, blocks], bs.at[p], br.at[p], device
             )
-            started(copy, to != row)
+            if is_other:
+                copy.start()
+            else:
+                started(copy, lead | (ty != y))
 
     act_frames(frames, frames + chip_frames, range(band))
     for copy, _, gets in x_margins[2:]:
@@ -362,8 +401,17 @@
     weight_piece(2)
     send_rows(2)
     act_frames(0, 1)
-    for k in (0, 1, 3, 4):
-        received(cot_margins[k][0], cot_margins[k][2])
+    weight_piece(3)
+    send_rows(3)
+    weight_piece(4)
+    send_rows(4)
+    weight_piece(5)
+    send_rows(5)
+
+    for copy, _, gets in cot_margins[3:]:
+        received(copy, gets)
+    received(cot_low, lead & row_low)
+    received(cot_high, lead & row_high)
     for t in range(2 * frames):
         for side, exists in ((0, row_low), (1, row_high)):
             keep = exists & has_next if t >= frames else exists
@@ -404,12 +452,7 @@
         biases = biases + folded(grad)
     gs1[tm, 0:1] = gains.sum(axis=0, keepdims=True)
     gs1[tm, 1:2] = biases.sum(axis=0, keepdims=True)
-    spread(gs1, tm, zc_peers(), 2)
-
-    weight_piece(3)
-    send_rows(3)
-    weight_piece(4)
-    send_rows(4)
+    collect(gs1, tm, column(1), 2)
 
     def of_piece(buf, count, p, send_sem, recv_sem):
         blocks = blocks_of(p)
@@ -418,16 +461,19 @@
     def send_z(p):
         blocks = blocks_of(p)
 
-        @pl.when(active)
+        @pl.when(follow)
         def _():
-            of_piece(brecv, n_rows - 1, p, bs, br).wait_recv()
+            received(of_piece(brecv, n_rows, p, bs, br), in_first_half)
+            received(of_piece(brecv, n_rows - 1, p, bs, br), jnp.logical_not(in_first_half))
             value = brecv[0, blocks].astype(F32)
             for k in range(1, n_rows):
                 value = value + brecv[k, blocks].astype(F32)
             crecv[z, blocks] = value.astype(BF16)
             mine = crecv.at[z, blocks]
-            for device in z_peers():
+            for device in column(1):
                 remote(mine, mine, zs.at[p], zr.at[p], device).start()
+
+    send_z(0)
 
     def shift_row(k, carry):
         t, h = k // high_rows, lax.rem(k, high_rows)
@@ -437,7 +483,7 @@
         return carry
 
     lax.fori_loop(0, 2 * frames * high_rows, shift_row, 0)
-    send_z(0)
+    send_z(1)
     sides = (a3.at[0], a0.at[pl.ds(frames * c, 2 * frames)], a3.at[1])
 
     def front_taps(a):
@@ -449,23 +495,20 @@
     one = front(frame(sides, 1), jnp.concatenate([front_taps(1), front_taps(0)], axis=1))
     cv[0:half] = front(frame(sides, 0), front_taps(0)) + one[:, :chans]
     cv[half:] = one[:, chans:]
-    send_z(1)
+    send_z(2)
     two = front(frame(sides, 2), jnp.concatenate([front_taps(2), front_taps(1)], axis=1))
     cv[0:half] += two[:, :chans]
     cv[half:] += front(frame(sides, 3), front_taps(2)) + two[:, chans:]
     for k in range(frames * band):
         v = xr[own + k // band, 1 + k % band].astype(F32)
         ofv[k // band, k % band] = (v + cv[k * WP : k * WP + width]).astype(BF16)
-    send_z(2)
-    gathered(gs1, 2).wait_recv()
-    gs2[row] = summed(gs1)
-    spread(gs2, row, xy_peers(), 3)
-
     send_z(3)
 
     send_z(4)
-
-    gathered(gs2, 3).wait_recv()
+    spread(gs2, row, gs1, (*plane(1), *plane(0)), 3)
+    send_z(5)
+
+    finished(gs2, 3)
     sums = summed(gs2)
     gain_grad, bias_grad = wide(sums[0:1]), wide(sums[1:2])
     gv[...] = sums[0:1]
@@ -486,7 +529,7 @@
         copy = remote(mine, mine, fs.at[p], fr.at[p], other)
         to_core.append(copy)
 
-        @pl.when(active)
+        @pl.when(follow)
         def _():
             of_piece(crecv, nz - 1, p, zs, zr).wait_recv()
             value = crecv[0, blocks].astype(F32)
@@ -498,35 +541,38 @@
     scale = 1.0 / math.sqrt(all_pixels)
     for p in range(N_PIECES):
         blocks = blocks_of(p)
-        received(to_core[p], jnp.logical_not(active))
+        received(to_core[p], lead)
         for m in range(blocks.start, blocks.stop):
             a, b = PAIRS[m // 3]
             at_m = (9 * a + 3 * b + m % 3) * chans
             wgv[:, at_m : at_m + chans] = fin[m] * scale
 
-    for slots, k in ((st1, 0), (st2, 1), (gs1, 2), (gs2, 3)):
-        gathered(slots, k).wait_send()
+    def parts_left(count, k, sends):
+        left(several(st1, count, st_s.at[k], st_r.at[k]), sends)
+
+    for k, chips in ((0, n_rows), (2, nz)):
+        parts_left(chips, k, lead)
+        parts_left(chips - 1, k, follow)
+    parts_left(2 * nz - 1, 1, follow)
+    parts_left(2 * n_rows - 1, 3, follow)
     partner_cot.wait_send()
     swapped_x.wait_send()
     for copy, sends, _ in (*cot_margins, *x_margins):
         left(copy, sends)
     left(gave_low, row_low)
     left(gave_high, row_high)
+    left(cot_low, follow & row_low)
+    left(cot_high, follow & row_high)
     left(passed_body, lead & has_before)
     left(passed_low, lead & has_before & row_low)
     left(passed_high, lead & has_before & row_high)
 
-    @pl.when(active)
-    def _():
-        for p in range(N_PIECES):
-            of_piece(bsend, dests - 1, p, bs, br).wait_send()
-            of_piece(crecv, nz - 1, p, zs, zr).wait_send()
-            to_core[p].wait_send()
-
-    @pl.when(jnp.logical_not(active))
-    def _():
-        for p in range(N_PIECES):
-            of_piece(bsend, dests, p, bs, br).wait_send()
+    own_half = follow & jnp.logical_not(in_first_half)
+    for p in range(N_PIECES):
+        left(of_piece(bsend, dests - 1, p, bs, br), own_half)
+        left(of_piece(bsend, dests, p, bs, br), jnp.logical_not(own_half))
+        left(of_piece(crecv, nz - 1, p, zs, zr), follow)
+        left(to_core[p], follow)
 
 
 def put_out(*refs):
@@ -564,12 +610,12 @@
         vmem((n_rows, 27, own_o, chans), BF16),
         vmem((nz, 27, own_o, chans), BF16),
         vmem((27, own_o, chans), F32),
-        vmem((n_rows, 2, chans), F32),
-        vmem((n_tm, 2, chans), F32),
+        vmem((n_rows * nc, 2, chans), F32),
+        vmem((nz, 2, chans), F32),
         vmem((n_tm, 2, chans), F32),
         vmem((n_rows, 2, chans), F32),
         dma((5,)),
-        dma((5,)), dma((5,)), dma((5,)), dma((5,)), dma((7,)), dma((7,)), dma((4,)), dma((4,)),
+        dma((5,)), dma((5,)), dma((5,)), dma((5,)), dma((9,)), dma((9,)), dma((4,)), dma((4,)),
         dma((N_PIECES,)), dma((N_PIECES,)), dma((N_PIECES,)), dma((N_PIECES,)),
         dma((N_PIECES,)), dma((N_PIECES,)),
     ]

time: 38.5 us -> 36.6 us (0.951)
  Pallas kernels: 37.8 us -> 35.8 us
    pallas_call x1, Pallas kernels: 37 us -> 35 us  [per_device(): pl.pallas_call(functools.partial(kernel, sizes), out_shape=(out(frames_in...]
where the time goes in v5:
time: 36.6 us; the launch traced here: 36.5 us
  Pallas kernels  35.8 us (98%)
  between operations  0.64 us (2%)
    pallas_call x1, Pallas kernels, per_device(): pl.pallas_call(functools.partial(kernel, sizes), out_shape=(out(frames_in...  35 us
    pallas_call x1, Pallas kernels, per_device(): pl.pallas_call(put_out, out_shape=[out(a.shape, a.dtype) for a in made],...  0.86 us

profile of v5, /device:TPU:1, one launch (start us, length us, event | category | flops | bytes accessed | tf_op | source)
XLA Modules:
  0.0 36.5 jit_solution(14182171418741984062)
XLA Ops:
  0.6 35.0 %block.1 = (bf16[2,4,120,128]{3,2,1,0:T(8,128)(2,1)S(1)}, bf16[2,4,120,128]{3,2,1,0:T(8,128)(2,1)S(1)}, f32[8,3456]{1,0:T(8,128)S(1)}, f32[1,128]{1,0:T(1,128)S(1)}, f32[1,128]{1,0:T(1,128)S(1)}) custom-call(bf16[2,4,120,128]{3,2,1,0:T(8,128)(2,1)} %x_hbm.1, f32[1,128]{1,0:T(1,128)} %bitcast.6, f32[1,128]{1,0:T(1,128)} %bitcast.7, ...), custom_call_target="tpu_custom_call" | custom-call | tf_op jit(solution)/shard_map/block/pallas_call | solution.py:633
  35.6 0.9 %put_out.1 = (bf16[2,4,120,128]{3,2,1,0:T(8,128)(2,1)}, bf16[2,4,120,128]{3,2,1,0:T(8,128)(2,1)}, f32[8,3456]{1,0:T(8,128)}, f32[1,128]{1,0:T(1,128)}, f32[1,128]{1,0:T(1,128)}) custom-call(bf16[2,4,120,128]{3,2,1,0:T(8,128)(2,1)S(1)} %get-tuple-element.15.refs_0_, bf16[2,4,120,128]{3,2,1,0:T(8,128)(2,1)S(1)} %get-tuple-element.16.refs_1_, ...), custom_call_target="tpu_custom_call" | custom-call | tf_op jit(solution)/shard_map/put_out/pallas_call | solution.py:650

commit v6 on v5

--- a/solution.py
+++ b/solution.py
@@ -38,7 +38,7 @@
 def kernel(
     sizes, x_hbm, gn_hbm, sh_hbm, w_hbm, cot_hbm,
     ofv, igv, wgv, gv, bv,
-    gain_ref, bias_ref, xr, cr, cpart, wv, a0, a3, c3, c3e, ct, ga, cv, bsend, brecv, crecv, fin,
+    gain_ref, bias_ref, xr, cr, cpart, wv, a0, a3, c3, ct, ga, cv, bsend, brecv, crecv, fin,
     st1, st2, gs1, gs2,
     load_sem, xs, xq, cs, cq, ps, pq, st_s, st_r, bs, br, zs, zr, fs, fr,
 ):
@@ -204,7 +204,7 @@
 
     partner_cot.start()
     swapped_x.start()
-    for copy, sends, _ in (*x_margins, *cot_margins):
+    for copy, sends, _ in (*x_margins[:3], *cot_margins, *x_margins[3:]):
         started(copy, sends)
 
     zeros_pad = jnp.zeros((WP - width, chans), F32)
@@ -281,7 +281,7 @@
         landing = cr.at[frames : 2 * frames, h]
         return remote(cr.at[0:frames, h], landing, ps.at[k], pq.at[k], other)
 
-    cot_low, cot_high = cot_corner(0, 7), cot_corner(band + 1, 8)
+    cot_low, cot_high = cot_corner(0, 5), cot_corner(band + 1, 6)
     for copy, _, gets in cot_margins[:2]:
         received(copy, gets)
     started(cot_low, follow & row_low)
@@ -296,6 +296,29 @@
     ga[0:half] += both[:, :chans]
     ga[half:] += back(frame(c3s, 3), back_taps(2)) + both[:, chans:]
 
+    def edge(t_in):
+        keep = has_next if t_in >= frames else True
+        for side, b, exists in ((0, 0, row_low), (1, 2, row_high)):
+            sides = three_ways(cr[t_in, side * (band + 1)], exists & keep)
+            lhs = jnp.concatenate([v.astype(BF16) for v in sides], axis=1)
+            gets = [(t, t_in - t) for t in range(frames) if 0 <= t_in - t < 3]
+            rhs = jnp.concatenate(
+                [
+                    jnp.concatenate(
+                        [wv[9 * (2 - a) + 3 * (2 - b) + 2 - s] for s in range(3)], axis=1
+                    )
+                    for _, a in gets
+                ],
+                axis=0,
+            )
+            given = back(lhs, rhs)
+            for j, (t, _) in enumerate(gets):
+                at_t = t * half + side * (band - 1) * WP
+                ga[at_t : at_t + WP] += given[:, j * chans : (j + 1) * chans]
+
+    for t in range(frames):
+        edge(t)
+
     finished(st2, 1)
     stats = summed(st2)
     wide = lambda v: jnp.broadcast_to(v, (8, chans))
@@ -308,6 +331,13 @@
     swapped_x.wait_recv()
     received(gave_low, row_low)
     received(gave_high, row_high)
+
+    for copy, _, gets in x_margins[2:]:
+        received(copy, gets)
+    started(passed_body, lead & has_before)
+    started(passed_low, lead & has_before & row_low)
+    started(passed_high, lead & has_before & row_high)
+
 
     def sigmoid(v):
         return 0.5 + 0.5 * jnp.tanh(0.5 * v)
@@ -374,7 +404,7 @@
             q = (ty - ys * c) * nx + tx
             device = {"z": z, "c": 1, "y": ty, "x": tx}
             copy = remote(
-                bsend.at[q, blocks], brecv.at[row, blocks], bs.at[p], br.at[p], device
+                bsend.at[q, blocks], brecv.at[row, blocks], bs.at[0], br.at[p], device
             )
             if is_other:
                 copy.start()
@@ -382,12 +412,6 @@
                 started(copy, lead | (ty != y))
 
     act_frames(frames, frames + chip_frames, range(band))
-    for copy, _, gets in x_margins[2:]:
-        received(copy, gets)
-    started(passed_body, lead & has_before)
-    started(passed_low, lead & has_before & row_low)
-    started(passed_high, lead & has_before & row_high)
-
     weight_piece(0)
     send_rows(0)
     act_frames(frames, frames + chip_frames, range(band, band + 2))
@@ -403,38 +427,12 @@
     act_frames(0, 1)
     weight_piece(3)
     send_rows(3)
-    weight_piece(4)
-    send_rows(4)
-    weight_piece(5)
-    send_rows(5)
-
     for copy, _, gets in cot_margins[3:]:
         received(copy, gets)
     received(cot_low, lead & row_low)
     received(cot_high, lead & row_high)
-    for t in range(2 * frames):
-        for side, exists in ((0, row_low), (1, row_high)):
-            keep = exists & has_next if t >= frames else exists
-            sides = three_ways(cr[t, side * (band + 1)], keep)
-            for shift in range(3):
-                c3e[shift, t, side] = sides[shift].astype(BF16)
-    for side, b in ((0, 0), (1, 2)):
-        lhs = jnp.concatenate(
-            [
-                jnp.concatenate(
-                    [c3e[s, t + a, side] for a in range(3) for s in range(3)], axis=1
-                )
-                for t in range(frames)
-            ],
-            axis=0,
-        )
-        rhs = jnp.concatenate(
-            [wv[9 * (2 - a) + 3 * (2 - b) + 2 - s] for a in range(3) for s in range(3)], axis=1
-        )
-        edge = back(lhs, rhs)
-        for t in range(frames):
-            at_t = t * half + side * (band - 1) * WP
-            ga[at_t : at_t + WP] += edge[t * WP : (t + 1) * WP]
+    for t in range(frames, 2 * frames):
+        edge(t)
 
     def pre_row(k):
         v = xr[own + k // band, 1 + k % band].astype(F32)
@@ -454,24 +452,28 @@
     gs1[tm, 1:2] = biases.sum(axis=0, keepdims=True)
     collect(gs1, tm, column(1), 2)
 
-    def of_piece(buf, count, p, send_sem, recv_sem):
-        blocks = blocks_of(p)
-        return several(buf.at[:, blocks], count, send_sem.at[p], recv_sem.at[p])
+    weight_piece(4)
+    send_rows(4)
+    weight_piece(5)
+    send_rows(5)
+
+    def of_piece(buf, count, p, recv_sem):
+        return several(buf.at[:, blocks_of(p)], count, bs.at[0], recv_sem.at[p])
 
     def send_z(p):
         blocks = blocks_of(p)
 
         @pl.when(follow)
         def _():
-            received(of_piece(brecv, n_rows, p, bs, br), in_first_half)
-            received(of_piece(brecv, n_rows - 1, p, bs, br), jnp.logical_not(in_first_half))
+            received(of_piece(brecv, n_rows, p, br), in_first_half)
+            received(of_piece(brecv, n_rows - 1, p, br), jnp.logical_not(in_first_half))
             value = brecv[0, blocks].astype(F32)
             for k in range(1, n_rows):
                 value = value + brecv[k, blocks].astype(F32)
             crecv[z, blocks] = value.astype(BF16)
             mine = crecv.at[z, blocks]
             for device in column(1):
-                remote(mine, mine, zs.at[p], zr.at[p], device).start()
+                remote(mine, mine, zs.at[0], zr.at[p], device).start()
 
     send_z(0)
 
@@ -502,10 +504,10 @@
     for k in range(frames * band):
         v = xr[own + k // band, 1 + k % band].astype(F32)
         ofv[k // band, k % band] = (v + cv[k * WP : k * WP + width]).astype(BF16)
+    spread(gs2, row, gs1, (*plane(1), *plane(0)), 3)
     send_z(3)
 
     send_z(4)
-    spread(gs2, row, gs1, (*plane(1), *plane(0)), 3)
     send_z(5)
 
     finished(gs2, 3)
@@ -522,30 +524,25 @@
         cot = cr[t, 1 + h].astype(F32)
         igv[t, h] = (inverse * (grad * gain - mean_dn - normed * mean_dnn) + cot).astype(BF16)
 
-    to_core = []
     for p in range(N_PIECES):
         blocks = blocks_of(p)
-        mine = fin.at[blocks]
-        copy = remote(mine, mine, fs.at[p], fr.at[p], other)
-        to_core.append(copy)
 
         @pl.when(follow)
         def _():
-            of_piece(crecv, nz - 1, p, zs, zr).wait_recv()
+            of_piece(crecv, nz - 1, p, zr).wait_recv()
             value = crecv[0, blocks].astype(F32)
             for k in range(1, nz):
                 value = value + crecv[k, blocks].astype(F32)
             fin[blocks] = value
-            copy.start()
-
+            remote(fin.at[blocks], fin.at[blocks], fs.at[0], fr.at[0], other).start()
+
+    whole = remote(fin, fin, fs.at[0], fr.at[0], other)
+    received(whole, lead)
     scale = 1.0 / math.sqrt(all_pixels)
-    for p in range(N_PIECES):
-        blocks = blocks_of(p)
-        received(to_core[p], lead)
-        for m in range(blocks.start, blocks.stop):
-            a, b = PAIRS[m // 3]
-            at_m = (9 * a + 3 * b + m % 3) * chans
-            wgv[:, at_m : at_m + chans] = fin[m] * scale
+    for m in range(27):
+        a, b = PAIRS[m // 3]
+        at_m = (9 * a + 3 * b + m % 3) * chans
+        wgv[:, at_m : at_m + chans] = fin[m] * scale
 
     def parts_left(count, k, sends):
         left(several(st1, count, st_s.at[k], st_r.at[k]), sends)
@@ -568,11 +565,10 @@
     left(passed_high, lead & has_before & row_high)
 
     own_half = follow & jnp.logical_not(in_first_half)
-    for p in range(N_PIECES):
-        left(of_piece(bsend, dests - 1, p, bs, br), own_half)
-        left(of_piece(bsend, dests, p, bs, br), jnp.logical_not(own_half))
-        left(of_piece(crecv, nz - 1, p, zs, zr), follow)
-        left(to_core[p], follow)
+    left(several(bsend, dests - 1, bs.at[0], br.at[0]), own_half)
+    left(several(bsend, dests, bs.at[0], br.at[0]), jnp.logical_not(own_half))
+    left(several(crecv, nz - 1, zs.at[0], zr.at[0]), follow)
+    left(whole, follow)
 
 
 def put_out(*refs):
@@ -602,7 +598,6 @@
         vmem((*chip, WP, chans), BF16),
         vmem((2, *rows, WP, chans), BF16),
         vmem((3, *rows, WP, chans), BF16),
-        vmem((3, 2 * frames, 2, WP, chans), BF16),
         vmem((nc, nc, 3 * chans // nc, frames * band * WP), BF16),
         vmem((frames * band * WP, chans), F32),
         vmem((frames * band * WP, chans), F32),
@@ -615,9 +610,8 @@
         vmem((n_tm, 2, chans), F32),
         vmem((n_rows, 2, chans), F32),
         dma((5,)),
-        dma((5,)), dma((5,)), dma((5,)), dma((5,)), dma((9,)), dma((9,)), dma((4,)), dma((4,)),
-        dma((N_PIECES,)), dma((N_PIECES,)), dma((N_PIECES,)), dma((N_PIECES,)),
-        dma((N_PIECES,)), dma((N_PIECES,)),
+        dma((5,)), dma((5,)), dma((5,)), dma((5,)), dma((7,)), dma((7,)), dma((4,)), dma((4,)),
+        dma((1,)), dma((N_PIECES,)), dma((1,)), dma((N_PIECES,)), dma((1,)), dma((1,)),
     ]
     anywhere = pl.BlockSpec(memory_space=pl.ANY)
     stays = pl.BlockSpec(memory_space=pltpu.HBM)

time: 36.6 us -> 36.4 us (level)
  no operation moved by 1% of the time
where the time goes in v6:
time: 36.4 us; the launch traced here: 36.3 us
  Pallas kernels  35.6 us (98%)
  between operations  0.64 us (2%)
    pallas_call x1, Pallas kernels, per_device(): pl.pallas_call(functools.partial(kernel, sizes), out_shape=(out(frames_in...  34.8 us
    pallas_call x1, Pallas kernels, per_device(): pl.pallas_call(put_out, out_shape=[out(a.shape, a.dtype) for a in made],...  0.86 us

profile of v6, /device:TPU:1, one launch (start us, length us, event | category | flops | bytes accessed | tf_op | source)
XLA Modules:
  0.0 36.3 jit_solution(14532372388838378160)
XLA Ops:
  0.6 34.8 %block.1 = (bf16[2,4,120,128]{3,2,1,0:T(8,128)(2,1)S(1)}, bf16[2,4,120,128]{3,2,1,0:T(8,128)(2,1)S(1)}, f32[8,3456]{1,0:T(8,128)S(1)}, f32[1,128]{1,0:T(1,128)S(1)}, f32[1,128]{1,0:T(1,128)S(1)}) custom-call(bf16[2,4,120,128]{3,2,1,0:T(8,128)(2,1)} %x_hbm.1, f32[1,128]{1,0:T(1,128)} %bitcast.6, f32[1,128]{1,0:T(1,128)} %bitcast.7, ...), custom_call_target="tpu_custom_call" | custom-call | tf_op jit(solution)/shard_map/block/pallas_call | solution.py:627
  35.4 0.9 %put_out.1 = (bf16[2,4,120,128]{3,2,1,0:T(8,128)(2,1)}, bf16[2,4,120,128]{3,2,1,0:T(8,128)(2,1)}, f32[8,3456]{1,0:T(8,128)}, f32[1,128]{1,0:T(1,128)}, f32[1,128]{1,0:T(1,128)}) custom-call(bf16[2,4,120,128]{3,2,1,0:T(8,128)(2,1)S(1)} %get-tuple-element.15.refs_0_, bf16[2,4,120,128]{3,2,1,0:T(8,128)(2,1)S(1)} %get-tuple-element.16.refs_1_, ...), custom_call_target="tpu_custom_call" | custom-call | tf_op jit(solution)/shard_map/put_out/pallas_call | solution.py:644

commit v7 on v6

--- a/solution.py
+++ b/solution.py
@@ -18,7 +18,7 @@
 F32 = jnp.float32
 BF16 = jnp.bfloat16
 PAIRS = tuple((a, b) for a in (2, 1, 0) for b in range(3))
-PIECES = ((0, 1), (1, 3), (3, 5), (5, 7), (7, 8), (8, 9))
+PIECES = ((0, 1), (1, 3), (3, 5), (5, 7), (7, 9))
 N_PIECES = len(PIECES)
 
 
@@ -40,7 +40,7 @@
     ofv, igv, wgv, gv, bv,
     gain_ref, bias_ref, xr, cr, cpart, wv, a0, a3, c3, ct, ga, cv, bsend, brecv, crecv, fin,
     st1, st2, gs1, gs2,
-    load_sem, xs, xq, cs, cq, ps, pq, st_s, st_r, bs, br, zs, zr, fs, fr,
+    load_sem, xs, xq, cs, cq, corner_s, corner_r, ps, pq, st_s, st_r, bs, br, zs, zr, fs, fr,
 ):
     nz, nc, ny, nx = sizes
     n_tm, n_rows = nz * nc, ny * nx
@@ -190,9 +190,11 @@
             (high, moved.at[:, 0], at(tm + way, row + 1), up_c & up_r, from_c & down_r),
             (low, moved.at[:, band + 1], at(tm + way, row - 1), up_c & down_r, from_c & up_r),
         ]
+        sems = [(send_sem.at[k], recv_sem.at[k]) for k in range(3)]
+        sems += [(corner_s.at[k], corner_r.at[k]) for k in range(2)]
         return [
-            (remote(src, dst, send_sem.at[k], recv_sem.at[k], device), sends, gets)
-            for k, (src, dst, device, sends, gets) in enumerate(plan)
+            (remote(src, dst, *sem, device), sends, gets)
+            for (src, dst, device, sends, gets), sem in zip(plan, sems)
         ]
 
     load_c.wait()
@@ -454,8 +456,6 @@
 
     weight_piece(4)
     send_rows(4)
-    weight_piece(5)
-    send_rows(5)
 
     def of_piece(buf, count, p, recv_sem):
         return several(buf.at[:, blocks_of(p)], count, bs.at[0], recv_sem.at[p])
@@ -508,7 +508,6 @@
     send_z(3)
 
     send_z(4)
-    send_z(5)
 
     finished(gs2, 3)
     sums = summed(gs2)
@@ -610,7 +609,7 @@
         vmem((n_tm, 2, chans), F32),
         vmem((n_rows, 2, chans), F32),
         dma((5,)),
-        dma((5,)), dma((5,)), dma((5,)), dma((5,)), dma((7,)), dma((7,)), dma((4,)), dma((4,)),
+        dma((3,)), dma((3,)), dma((3,)), dma((3,)), dma((2,)), dma((2,)), dma((7,)), dma((7,)), dma((4,)), dma((4,)),
         dma((1,)), dma((N_PIECES,)), dma((1,)), dma((N_PIECES,)), dma((1,)), dma((1,)),
     ]
     anywhere = pl.BlockSpec(memory_space=pl.ANY)

time: 36.4 us -> 36 us (0.989)
  Pallas kernels: 35.6 us -> 35.2 us
    pallas_call x1, Pallas kernels: 34.8 us -> 34.4 us  [per_device(): pl.pallas_call(functools.partial(kernel, sizes), out_shape=(out(frames_in...]
where the time goes in v7:
time: 36 us; the launch traced here: 35.9 us
  Pallas kernels  35.2 us (98%)
  between operations  0.64 us (2%)
    pallas_call x1, Pallas kernels, per_device(): pl.pallas_call(functools.partial(kernel, sizes), out_shape=(out(frames_in...  34.4 us
    pallas_call x1, Pallas kernels, per_device(): pl.pallas_call(put_out, out_shape=[out(a.shape, a.dtype) for a in made],...  0.86 us

profile of v7, /device:TPU:1, one launch (start us, length us, event | category | flops | bytes accessed | tf_op | source)
XLA Modules:
  0.0 35.9 jit_solution(3801645229700488421)
XLA Ops:
  0.6 34.4 %block.1 = (bf16[2,4,120,128]{3,2,1,0:T(8,128)(2,1)S(1)}, bf16[2,4,120,128]{3,2,1,0:T(8,128)(2,1)S(1)}, f32[8,3456]{1,0:T(8,128)S(1)}, f32[1,128]{1,0:T(1,128)S(1)}, f32[1,128]{1,0:T(1,128)S(1)}) custom-call(bf16[2,4,120,128]{3,2,1,0:T(8,128)(2,1)} %x_hbm.1, f32[1,128]{1,0:T(1,128)} %bitcast.6, f32[1,128]{1,0:T(1,128)} %bitcast.7, ...), custom_call_target="tpu_custom_call" | custom-call | tf_op jit(solution)/shard_map/block/pallas_call | solution.py:626
  35.0 0.9 %put_out.1 = (bf16[2,4,120,128]{3,2,1,0:T(8,128)(2,1)}, bf16[2,4,120,128]{3,2,1,0:T(8,128)(2,1)}, f32[8,3456]{1,0:T(8,128)}, f32[1,128]{1,0:T(1,128)}, f32[1,128]{1,0:T(1,128)}) custom-call(bf16[2,4,120,128]{3,2,1,0:T(8,128)(2,1)S(1)} %get-tuple-element.15.refs_0_, bf16[2,4,120,128]{3,2,1,0:T(8,128)(2,1)S(1)} %get-tuple-element.16.refs_1_, ...), custom_call_target="tpu_custom_call" | custom-call | tf_op jit(solution)/shard_map/put_out/pallas_call | solution.py:643

commit v8 on v7

--- a/solution.py
+++ b/solution.py
@@ -429,6 +429,9 @@
     act_frames(0, 1)
     weight_piece(3)
     send_rows(3)
+    weight_piece(4)
+    send_rows(4)
+
     for copy, _, gets in cot_margins[3:]:
         received(copy, gets)
     received(cot_low, lead & row_low)
@@ -454,9 +457,6 @@
     gs1[tm, 1:2] = biases.sum(axis=0, keepdims=True)
     collect(gs1, tm, column(1), 2)
 
-    weight_piece(4)
-    send_rows(4)
-
     def of_piece(buf, count, p, recv_sem):
         return several(buf.at[:, blocks_of(p)], count, bs.at[0], recv_sem.at[p])
 
@@ -504,10 +504,10 @@
     for k in range(frames * band):
         v = xr[own + k // band, 1 + k % band].astype(F32)
         ofv[k // band, k % band] = (v + cv[k * WP : k * WP + width]).astype(BF16)
+    send_z(3)
+
+    send_z(4)
     spread(gs2, row, gs1, (*plane(1), *plane(0)), 3)
-    send_z(3)
-
-    send_z(4)
 
     finished(gs2, 3)
     sums = summed(gs2)

time: 36 us -> 36.1 us (level)
  no operation moved by 1% of the time
where the time goes in v8:
time: 36.1 us; the launch traced here: 36 us
  Pallas kernels  35.3 us (98%)
  between operations  0.64 us (2%)
    pallas_call x1, Pallas kernels, per_device(): pl.pallas_call(functools.partial(kernel, sizes), out_shape=(out(frames_in...  34.5 us
    pallas_call x1, Pallas kernels, per_device(): pl.pallas_call(put_out, out_shape=[out(a.shape, a.dtype) for a in made],...  0.86 us

profile of v8, /device:TPU:1, one launch (start us, length us, event | category | flops | bytes accessed | tf_op | source)
XLA Modules:
  0.0 36.0 jit_solution(4163352434519541333)
XLA Ops:
  0.6 34.5 %block.1 = (bf16[2,4,120,128]{3,2,1,0:T(8,128)(2,1)S(1)}, bf16[2,4,120,128]{3,2,1,0:T(8,128)(2,1)S(1)}, f32[8,3456]{1,0:T(8,128)S(1)}, f32[1,128]{1,0:T(1,128)S(1)}, f32[1,128]{1,0:T(1,128)S(1)}) custom-call(bf16[2,4,120,128]{3,2,1,0:T(8,128)(2,1)} %x_hbm.1, f32[1,128]{1,0:T(1,128)} %bitcast.6, f32[1,128]{1,0:T(1,128)} %bitcast.7, ...), custom_call_target="tpu_custom_call" | custom-call | tf_op jit(solution)/shard_map/block/pallas_call | solution.py:626
  35.1 0.9 %put_out.1 = (bf16[2,4,120,128]{3,2,1,0:T(8,128)(2,1)}, bf16[2,4,120,128]{3,2,1,0:T(8,128)(2,1)}, f32[8,3456]{1,0:T(8,128)}, f32[1,128]{1,0:T(1,128)}, f32[1,128]{1,0:T(1,128)}) custom-call(bf16[2,4,120,128]{3,2,1,0:T(8,128)(2,1)S(1)} %get-tuple-element.15.refs_0_, bf16[2,4,120,128]{3,2,1,0:T(8,128)(2,1)S(1)} %get-tuple-element.16.refs_1_, ...), custom_call_target="tpu_custom_call" | custom-call | tf_op jit(solution)/shard_map/put_out/pallas_call | solution.py:643

commit v9 on v7

--- a/solution.py
+++ b/solution.py
@@ -147,10 +147,10 @@
     pl.semaphore_wait(barrier, partners)
 
     def summed(slots):
-        total = slots[0]
-        for k in range(1, slots.shape[0]):
-            total = total + slots[k]
-        return total
+        parts = [slots[k] for k in range(slots.shape[0])]
+        while len(parts) > 1:
+            parts = [low + high for low, high in zip(parts[::2], parts[1::2])]
+        return parts[0]
 
     def collect(slots, mine, peers, k):
         part = slots.at[mine]

time: 36 us -> 35.9 us (level)
  no operation moved by 1% of the time
where the time goes in v9:
time: 35.9 us; the launch traced here: 35.8 us
  Pallas kernels  35.2 us (98%)
  between operations  0.64 us (2%)
    pallas_call x1, Pallas kernels, per_device(): pl.pallas_call(functools.partial(kernel, sizes), out_shape=(out(frames_in...  34.3 us
    pallas_call x1, Pallas kernels, per_device(): pl.pallas_call(put_out, out_shape=[out(a.shape, a.dtype) for a in made],...  0.86 us

profile of v9, /device:TPU:1, one launch (start us, length us, event | category | flops | bytes accessed | tf_op | source)
XLA Modules:
  0.0 35.8 jit_solution(5163641139642103998)
XLA Ops:
  0.6 34.3 %block.1 = (bf16[2,4,120,128]{3,2,1,0:T(8,128)(2,1)S(1)}, bf16[2,4,120,128]{3,2,1,0:T(8,128)(2,1)S(1)}, f32[8,3456]{1,0:T(8,128)S(1)}, f32[1,128]{1,0:T(1,128)S(1)}, f32[1,128]{1,0:T(1,128)S(1)}) custom-call(bf16[2,4,120,128]{3,2,1,0:T(8,128)(2,1)} %x_hbm.1, f32[1,128]{1,0:T(1,128)} %bitcast.6, f32[1,128]{1,0:T(1,128)} %bitcast.7, ...), custom_call_target="tpu_custom_call" | custom-call | tf_op jit(solution)/shard_map/block/pallas_call | solution.py:626
  35.0 0.9 %put_out.1 = (bf16[2,4,120,128]{3,2,1,0:T(8,128)(2,1)}, bf16[2,4,120,128]{3,2,1,0:T(8,128)(2,1)}, f32[8,3456]{1,0:T(8,128)}, f32[1,128]{1,0:T(1,128)}, f32[1,128]{1,0:T(1,128)}) custom-call(bf16[2,4,120,128]{3,2,1,0:T(8,128)(2,1)S(1)} %get-tuple-element.15.refs_0_, bf16[2,4,120,128]{3,2,1,0:T(8,128)(2,1)S(1)} %get-tuple-element.16.refs_1_, ...), custom_call_target="tpu_custom_call" | custom-call | tf_op jit(solution)/shard_map/put_out/pallas_call | solution.py:643
